TPU v7x, 512 devices: a whole 4x4x16 slice. The times are simulated.
512 devices in a mesh: lat: 16 (over y, x_lo, core), lon: 32 (over x_hi, z).
Axes of the slice: x: 4 (x_hi: 2, x_lo: 2; x = x_hi * 2 + x_lo), y: 4, z: 16, core: 2. Of those that a mesh axis runs over, the one named last changes fastest.
Arguments:
- ensemble: bfloat16 [128, 512, 2048], P('lat', 'lon'), may hold values from -6 to 6
- channel_weights: bfloat16 [16, 32, 32, 32, 128], P('lat', 'lon'), may hold values from -1 to 1
- block_column: int32 [16, 32, 32], P('lat', 'lon'), may hold values from 0 to 127
- innovation: bfloat16 [16, 32, 32, 128], P('lat', 'lon'), may hold values from -6 to 6
- error_precision: bfloat16 [16, 32, 32, 128], P('lat', 'lon'), may hold values from 0.25 to 4
- block_count: int32 [16, 32], P('lat', 'lon'), may hold values from 1 to 32, as said below
- neighbours: int32 [64, 256, 12], P('lat', 'lon'), may hold values from 0 to 287
Outputs:
- analysis: bfloat16 [128, 512, 2048], P('lat', 'lon')
Inputs may be any that keep to these rules, and one draw needn't show every extreme that they name: The live blocks of a tile are its first block_count slots; at least one tile fills all 32 slots.
All inputs are finite; a program needn't handle non-finite values.
Results may differ from a plain program's by a relative error of at most 0.0074.
Values may be sent and summed in bfloat16 or wider, within the bound.
A program may use at most 64 MiB of HBM per device.

v0:
```python
import jax
import jax.numpy as jnp
from jax import lax
from jax.sharding import PartitionSpec as P

NSI = 6
LOC = 12


def padded(block, sides, width, periodic):
    for axis, dim in sides:
        count = lax.axis_size(axis)
        forward = [(i, i + 1) for i in range(count - 1)]
        if periodic:
            forward.append((count - 1, 0))
        backward = [(target, source) for source, target in forward]
        low = lax.ppermute(
            lax.slice_in_dim(block, block.shape[dim] - width, None, axis=dim), axis, forward
        )
        high = lax.ppermute(lax.slice_in_dim(block, 0, width, axis=dim), axis, backward)
        block = jnp.concatenate([low, block, high], axis=dim)
    return block


def from_behind(block, axis, distance):
    devices = range(lax.axis_size(axis))
    route = [(i - distance, i) for i in devices if i - distance in devices]
    return lax.ppermute(block, axis, route)


def passed_along(value, axis, steps):
    count = lax.axis_size(axis)
    pairs = [(source, (source + steps) % count) for source in range(count)]
    return lax.ppermute(value, axis, pairs)


def newton_schulz(gram_matrix, projected):
    members = gram_matrix.shape[-1]
    identity = jnp.eye(members, dtype=jnp.float32)
    frobenius = jnp.sqrt(jnp.sum(gram_matrix * gram_matrix, axis=(1, 2)))
    current = gram_matrix / frobenius[:, None, None]
    inverse = jnp.broadcast_to(identity, gram_matrix.shape)
    for turn_index in range(NSI):
        middle = 1.5 * identity - 0.5 * jnp.einsum(
            "pij,pjk->pik", inverse, current, precision=lax.Precision.HIGHEST
        )
        current = jnp.einsum("pij,pjk->pik", current, middle, precision=lax.Precision.HIGHEST)
        inverse = jnp.einsum("pij,pjk->pik", middle, inverse, precision=lax.Precision.HIGHEST)
    root_scale = jnp.sqrt(frobenius)
    spread_part = inverse * (jnp.sqrt(jnp.float32(members - 1.0)) / root_scale)[:, None, None]
    halfway = jnp.einsum("pij,pj->pi", inverse, projected, precision=lax.Precision.HIGHEST)
    mean_shift = (
        jnp.einsum("pij,pj->pi", inverse, halfway, precision=lax.Precision.HIGHEST)
        / frobenius[:, None]
    )
    return (spread_part + mean_shift[:, :, None]).astype(jnp.bfloat16)


def body(
    ensemble, channel_weights, block_column, innovation, error_precision, block_count, neighbours
):
    lat_rows, lon_cols, row_width = ensemble.shape
    slot_count = block_column.shape[2]
    levels = channel_weights.shape[3]
    block_len = channel_weights.shape[4]
    members = row_width // levels
    coarse_lat = neighbours.shape[0]
    coarse_lon = neighbours.shape[1]
    columns = block_column[0, 0]
    state_cols = ensemble.reshape(lat_rows * lon_cols, levels, members)
    picked = state_cols[columns].astype(jnp.float32)
    average = jnp.mean(picked, axis=2, keepdims=True)
    anomaly = (picked - average).astype(jnp.bfloat16)
    blocks = jnp.einsum(
        "blk,blo->bko", anomaly, channel_weights[0, 0], preferred_element_type=jnp.float32
    ).astype(jnp.bfloat16)
    live_mask = (jnp.arange(slot_count, dtype=jnp.int32) < block_count[0, 0]).astype(jnp.bfloat16)
    weighted = error_precision[0, 0] * live_mask[:, None]
    position = jnp.stack(
        [(columns // lon_cols).astype(jnp.bfloat16), (columns % lon_cols).astype(jnp.bfloat16)], 1
    )
    position_row = jnp.concatenate(
        [position, jnp.zeros((slot_count, block_len - 2), jnp.bfloat16)], 1
    )
    facts = jnp.stack([innovation[0, 0], weighted, position_row], 1)
    packed = jnp.concatenate([blocks, facts], 1)[None, None]
    packed = padded(packed, (("lat", 0),), 1, False)
    packed = padded(packed, (("lon", 1),), 1, True)
    flat_packed = packed.reshape(9 * slot_count, members + 3, block_len)
    flat_blocks = flat_packed[:, :members]
    flat_facts = flat_packed[:, members:].astype(jnp.float32)
    offset = jnp.arange(9 * slot_count, dtype=jnp.int32) // slot_count
    north_south = (offset // 3 - 1).astype(jnp.float32) * lat_rows + flat_facts[:, 2, 0]
    east_west = (offset % 3 - 1).astype(jnp.float32) * lon_cols + flat_facts[:, 2, 1]
    point_cols = 2.0 * jnp.arange(coarse_lon, dtype=jnp.int32).astype(jnp.float32)[:, None]

    def coarse_row(pieces):
        row_index, listed = pieces
        chosen = flat_blocks[listed]
        delta_lat = north_south[listed] - 2.0 * row_index.astype(jnp.float32)
        delta_lon = east_west[listed] - point_cols
        taper = jnp.exp(-(delta_lat * delta_lat + delta_lon * delta_lon) / (2.0 * LOC * LOC))
        root_weight = jnp.sqrt(taper[:, :, None] * flat_facts[listed, 1])
        scaled = (root_weight[:, :, None, :] * chosen).astype(jnp.bfloat16)
        forced = (root_weight * flat_facts[listed, 0]).astype(jnp.bfloat16)
        gram_matrix = jnp.einsum(
            "pjko,pjlo->pkl", scaled, scaled, preferred_element_type=jnp.float32
        ) + (members - 1.0) * jnp.eye(members, dtype=jnp.float32)
        projected = jnp.einsum("pjko,pjo->pk", scaled, forced, preferred_element_type=jnp.float32)
        return newton_schulz(gram_matrix, projected)

    coarse = lax.map(coarse_row, (jnp.arange(coarse_lat, dtype=jnp.int32), neighbours))
    coarse_flat = coarse.reshape(coarse_lat, coarse_lon, members * members)
    below = from_behind(coarse_flat[:1], "lat", -1)
    ending = lax.axis_index("lat") == lax.axis_size("lat") - 1
    below = jnp.where(ending, coarse_flat[-1:], below)
    extended = jnp.concatenate([coarse_flat, below], 0)
    beside = passed_along(extended[:, :1], "lon", -1)
    coarse_ext = jnp.concatenate([extended, beside], 1).astype(jnp.float32)
    row_even = coarse_ext[:-1]
    row_odd = 0.5 * (coarse_ext[:-1] + coarse_ext[1:])
    fine_rows = jnp.stack([row_even, row_odd], 1).reshape(
        lat_rows, coarse_lon + 1, members * members
    )
    col_even = fine_rows[:, :-1]
    col_odd = 0.5 * (fine_rows[:, :-1] + fine_rows[:, 1:])
    blended = (
        jnp.stack([col_even, col_odd], 2)
        .reshape(lat_rows, lon_cols, members, members)
        .astype(jnp.bfloat16)
    )
    state_full = ensemble.reshape(lat_rows, lon_cols, levels, members).astype(jnp.float32)
    center = jnp.mean(state_full, axis=3, keepdims=True)
    spread = (state_full - center).astype(jnp.bfloat16)
    result = center + jnp.einsum(
        "rclk,rckj->rclj", spread, blended, preferred_element_type=jnp.float32
    )
    return result.astype(jnp.bfloat16).reshape(lat_rows, lon_cols, row_width)


def solution(mesh):
    return jax.shard_map(
        body,
        mesh=mesh,
        in_specs=(
            P("lat", "lon", None),
            P("lat", "lon", None, None, None),
            P("lat", "lon", None),
            P("lat", "lon", None, None),
            P("lat", "lon", None, None),
            P("lat", "lon"),
            P("lat", "lon", None),
        ),
        out_specs=P("lat", "lon", None),
        check_vma=False,
    )
```

profile of v0, /device:TPU:1, one launch (start us, length us, event | category | flops | bytes accessed | tf_op | source)
XLA Modules:
  0.0 195.0 jit_solution(13449531918205466477)
XLA Ops:
  0.7 2.1 %reshape.291 = bf16[128,32,64]{2,1,0:T(8,128)(2,1)S(1)} reshape(bf16[8,16,2048]{2,1,0:T(8,128)(2,1)} %param.9) | data formatting | bytes 1048576 | tf_op jit(solution)/shard_map/reshape | solution.py:70
  5.7 4.5 %collective-permute-start = (bf16[1,1,32,67,128]{4,2,3,1,0:T(8,128)(2,1)S(1)}, bf16[1,1,32,67,128]{4,2,3,1,0:T(8,128)(2,1)S(1)}, u32[]{:S(2)}, u32[]{:S(2)}) collective-permute-start(bf16[1,1,32,67,128]{4,2,3,1,0:T(8,128)(2,1)S(1)} %copy.30), channel_id=1, source_target_pairs={{0,32},{32,64},{64,96},{96,128},{128,160},{160,192},{192,224},{224... | collective-permute-start | bytes 1646600 | tf_op jit(solution)/shard_map/ppermute | solution.py:17
  10.2 5.6 %collective-permute-start.1 = (bf16[1,1,32,67,128]{4,2,3,1,0:T(8,128)(2,1)S(1)}, bf16[1,1,32,67,128]{4,2,3,1,0:T(8,128)(2,1)S(1)}, u32[]{:S(2)}, u32[]{:S(2)}) collective-permute-start(bf16[1,1,32,67,128]{4,2,3,1,0:T(8,128)(2,1)S(1)} %copy.30), channel_id=1, source_target_pairs={{32,0},{64,32},{96,64},{128,96},{160,128},{192,160},{224,192},{256... | collective-permute-start | bytes 1646600 | tf_op jit(solution)/shard_map/ppermute | solution.py:20
  16.8 7.4 %collective-permute-done.1 = bf16[1,1,32,67,128]{4,2,3,1,0:T(8,128)(2,1)S(1)} collective-permute-done((bf16[1,1,32,67,128]{4,2,3,1,0:T(8,128)(2,1)S(1)}, bf16[1,1,32,67,128]{4,2,3,1,0:T(8,128)(2,1)S(1)}, u32[]{:S(2)}, u32[]{:S(2)}) %collective-permute-start.1) | collective-permute-done | bytes 548896 | tf_op jit(solution)/shard_map/ppermute | solution.py:20
  24.6 1.4 copy.34
  26.1 3.9 %collective-permute-start.2 = (bf16[3,1,32,67,128]{4,2,3,1,0:T(8,128)(2,1)}, bf16[3,1,32,67,128]{4,2,3,1,0:T(8,128)(2,1)}, u32[]{:S(2)}, u32[]{:S(2)}) collective-permute-start(bf16[3,1,32,67,128]{4,2,3,1,0:T(8,128)(2,1)} %copy.34), channel_id=1, source_target_pairs={{0,1},{1,2},{2,3},{3,4},{4,5},{5,6},{6,7},{7,8},{8,9},{9,10},{10,1... | collective-permute-start | bytes 4939784 | tf_op jit(solution)/shard_map/ppermute | solution.py:17
  30.0 12.0 %collective-permute-start.3 = (bf16[3,1,32,67,128]{4,2,3,1,0:T(8,128)(2,1)}, bf16[3,1,32,67,128]{4,2,3,1,0:T(8,128)(2,1)}, u32[]{:S(2)}, u32[]{:S(2)}) collective-permute-start(bf16[3,1,32,67,128]{4,2,3,1,0:T(8,128)(2,1)} %copy.34), channel_id=1, source_target_pairs={{1,0},{2,1},{3,2},{4,3},{5,4},{6,5},{7,6},{8,7},{9,8},{10,9},{11,1... | collective-permute-start | bytes 4939784 | tf_op jit(solution)/shard_map/ppermute | solution.py:20
  42.0 24.0 %collective-permute-done.2 = bf16[3,1,32,67,128]{4,2,3,1,0:T(8,128)(2,1)} collective-permute-done((bf16[3,1,32,67,128]{4,2,3,1,0:T(8,128)(2,1)}, bf16[3,1,32,67,128]{4,2,3,1,0:T(8,128)(2,1)}, u32[]{:S(2)}, u32[]{:S(2)}) %collective-permute-start.2) | collective-permute-done | bytes 1646624 | tf_op jit(solution)/shard_map/ppermute | solution.py:17
  66.0 2.1 %copy.36 = bf16[3,1,32,67,128]{4,3,2,1,0:T(8,128)(2,1)S(1)} copy(bf16[3,1,32,67,128]{4,2,3,1,0:T(8,128)(2,1)} %collective-permute-done.2) | data formatting | bytes 3293184 | tf_op jit(solution)/shard_map/ppermute | solution.py:17
  68.1 2.1 %copy.37 = bf16[3,1,32,67,128]{4,3,2,1,0:T(8,128)(2,1)S(1)} copy(bf16[3,1,32,67,128]{4,2,3,1,0:T(8,128)(2,1)} %collective-permute-done.3) | data formatting | bytes 3293184 | tf_op jit(solution)/shard_map/ppermute | solution.py:20
  70.2 1.7 pad_maximum_fusion
  71.9 3.5 %slice.69 = bf16[288,64,128]{2,1,0:T(8,128)(2,1)} slice(bf16[288,67,128]{2,1,0:T(8,128)(2,1)S(1)} %bitcast.213), slice={[0:288], [0:64], [0:128]} | slice | bytes 9437184 | tf_op jit(solution)/shard_map/slice | solution.py:90
  75.5 2.9 %slice_reduce_fusion = (f32[288]{0:T(512)S(1)}, f32[288]{0:T(512)S(1)}) fusion(f32[288,3,128]{2,1,0:T(4,128)S(1)} %slice_convert_fusion.1), kind=kLoop, calls=%fused_computation.79 | loop fusion | bytes 4608 | tf_op jit(solution)/shard_map/slice | solution.py:94
  78.5 82.6 %while.11 = (s32[]{:T(128)}, bf16[4,8,64,64]{3,2,1,0:T(8,128)(2,1)S(1)}, s32[4,8,12]{2,1,0:T(8,128)}, f32[288]{0:T(512)S(1)}, s32[4]{0:T(128)S(1)}, /*index=5*/f...) while((s32[]{:T(128)}, ...), condition=%wide.region_4.5_spmd.clone, body=%wide.region_2.4_spmd.clone.sunk | while | flops 536280000 | bytes 14421297 | solution.py:112
  83.6 1.4 gather_fusion.2
  85.0 1.4 gather_fusion.1
  86.5 3.2 %gather_fusion = bf16[96,64,128]{2,1,0:T(8,128)(2,1)S(1)} fusion(bf16[288,64,128]{2,1,0:T(8,128)(2,1)} %get-tuple-element.222, s32[1024]{0:T(1024)S(1)} %pad_clamp_fusion.3), kind=kCustom, calls=%fused_computation.3.clone.clone.1 | custom fusion | bytes 3146112 | tf_op jit(solution)/shard_map/while/body/eval_jaxpr/gather | solution.py:99
  104.2 1.4 gather_fusion.2
  105.7 1.4 gather_fusion.1
  107.1 3.2 %gather_fusion = bf16[96,64,128]{2,1,0:T(8,128)(2,1)S(1)} fusion(bf16[288,64,128]{2,1,0:T(8,128)(2,1)} %get-tuple-element.222, s32[1024]{0:T(1024)S(1)} %pad_clamp_fusion.3), kind=kCustom, calls=%fused_computation.3.clone.clone.1 | custom fusion | bytes 3146112 | tf_op jit(solution)/shard_map/while/body/eval_jaxpr/gather | solution.py:99
  124.8 1.4 gather_fusion.2
  126.3 1.4 gather_fusion.1
  127.7 3.2 %gather_fusion = bf16[96,64,128]{2,1,0:T(8,128)(2,1)S(1)} fusion(bf16[288,64,128]{2,1,0:T(8,128)(2,1)} %get-tuple-element.222, s32[1024]{0:T(1024)S(1)} %pad_clamp_fusion.3), kind=kCustom, calls=%fused_computation.3.clone.clone.1 | custom fusion | bytes 3146112 | tf_op jit(solution)/shard_map/while/body/eval_jaxpr/gather | solution.py:99
  145.4 1.4 gather_fusion.2
  148.4 3.2 %gather_fusion = bf16[96,64,128]{2,1,0:T(8,128)(2,1)S(1)} fusion(bf16[288,64,128]{2,1,0:T(8,128)(2,1)} %get-tuple-element.222, s32[1024]{0:T(1024)S(1)} %pad_clamp_fusion.3), kind=kCustom, calls=%fused_computation.3.clone.clone.1 | custom fusion | bytes 3146112 | tf_op jit(solution)/shard_map/while/body/eval_jaxpr/gather | solution.py:99
  161.9 2.1 %collective-permute-start.4 = (bf16[1,8,4096]{2,1,0:T(8,128)(2,1)}, bf16[1,8,4096]{2,1,0:T(8,128)(2,1)}, u32[]{:S(2)}, u32[]{:S(2)}) collective-permute-start(bf16[1,8,4096]{2,1,0:T(8,128)(2,1)} %slice.48), channel_id=1, source_target_pairs={{32,0},{64,32},{96,64},{128,96},{160,128},{192,160},{224,192},{256... | collective-permute-start | bytes 196616 | tf_op jit(solution)/shard_map/ppermute | solution.py:28
  166.3 9.3 %collective-permute-done.4 = bf16[1,8,4096]{2,1,0:T(8,128)(2,1)} collective-permute-done((bf16[1,8,4096]{2,1,0:T(8,128)(2,1)}, bf16[1,8,4096]{2,1,0:T(8,128)(2,1)}, u32[]{:S(2)}, u32[]{:S(2)}) %collective-permute-start.4) | collective-permute-done | bytes 65568 | tf_op jit(solution)/shard_map/ppermute | solution.py:28
  176.5 8.0 %collective-permute-start.5 = (bf16[5,1,4096]{2,1,0:T(2,128)(2,1)S(1)}, bf16[5,1,4096]{2,1,0:T(2,128)(2,1)S(1)}, u32[]{:S(2)}, u32[]{:S(2)}) collective-permute-start(bf16[5,1,4096]{2,1,0:T(2,128)(2,1)S(1)} %pad_maximum_fusion.4), channel_id=1, source_target_pairs={{0,31},{1,0},{2,1},{3,2},{4,3},{5,4},{6,5},{7,6},{8,7},{9,8},{10,9... | collective-permute-start | bytes 122888 | tf_op jit(solution)/shard_map/ppermute | solution.py:34
  184.5 1.4 collective-permute-done.5
  187.9 2.4 %convert_element_type.110 = bf16[8,16,64,64]{3,2,1,0:T(8,128)(2,1)} reshape(bf16[8,8,2,4096]{3,2,1,0:T(2,128)(2,1)S(1)} %copy.40) | data formatting | bytes 2097152 | tf_op jit(solution)/shard_map/convert_element_type | solution.py:130
  190.3 3.1 %add_convert_fusion.1 = bf16[8,16,32,64]{3,2,1,0:T(8,128)(2,1)S(1)} fusion(bf16[8,16,64,64]{3,2,1,0:T(8,128)(2,1)} %convert_element_type.110, f32[8,16,32,64]{3,2,1,0:T(8,128)S(1)} %reshape.296, f32[8,16,32]{2,1,0:T(8,128)S(1)} %broadcast_multiply_fusion), kind=kOutput, calls=%fused_computation.55 | convolution fusion | flops 34603008 | bytes 2637824 | tf_op jit(solution)/shard_map/rclk,rckj->rclj/dot_general | solution.py:135
  193.4 1.6 reshape.295
  (228 shorter events, 66.9 us)
Async XLA Ops:
  0.0 4.7 %copy-start = (bf16[1,1,32,32,128]{4,3,2,1,0:T(8,128)(2,1)S(1)}, bf16[1,1,32,32,128]{4,3,2,1,0:T(8,128)(2,1)}, u32[]{:S(2)}) copy-start(bf16[1,1,32,32,128]{4,3,2,1,0:T(8,128)(2,1)} %param.10) | copy-start | bytes 786436
  0.0 4.7 %copy-start.2 = (bf16[1,1,32,128]{3,2,1,0:T(8,128)(2,1)S(1)}, bf16[1,1,32,128]{3,2,1,0:T(8,128)(2,1)}, u32[]{:S(2)}) copy-start(bf16[1,1,32,128]{3,2,1,0:T(8,128)(2,1)} %param.12) | copy-start | bytes 24580
  0.7 4.7 %copy-start.3 = (bf16[1,1,32,128]{3,2,1,0:T(8,128)(2,1)S(1)}, bf16[1,1,32,128]{3,2,1,0:T(8,128)(2,1)}, u32[]{:S(2)}) copy-start(bf16[1,1,32,128]{3,2,1,0:T(8,128)(2,1)} %param.13) | copy-start | bytes 24580
  5.7 10.9 %collective-permute-start = (bf16[1,1,32,67,128]{4,2,3,1,0:T(8,128)(2,1)S(1)}, bf16[1,1,32,67,128]{4,2,3,1,0:T(8,128)(2,1)S(1)}, u32[]{:S(2)}, u32[]{:S(2)}) collective-permute-start(bf16[1,1,32,67,128]{4,2,3,1,0:T(8,128)(2,1)S(1)} %copy.30), channel_id=1, source_target_pairs={{0,32},{32,64},{64,96},{96,128},{128,160},{160,192},{192,224},{224... | collective-permute-start | bytes 1646600 | tf_op jit(solution)/shard_map/ppermute | solution.py:17
  10.2 14.0 %collective-permute-start.1 = (bf16[1,1,32,67,128]{4,2,3,1,0:T(8,128)(2,1)S(1)}, bf16[1,1,32,67,128]{4,2,3,1,0:T(8,128)(2,1)S(1)}, u32[]{:S(2)}, u32[]{:S(2)}) collective-permute-start(bf16[1,1,32,67,128]{4,2,3,1,0:T(8,128)(2,1)S(1)} %copy.30), channel_id=1, source_target_pairs={{32,0},{64,32},{96,64},{128,96},{160,128},{192,160},{224,192},{256... | collective-permute-start | bytes 1646600 | tf_op jit(solution)/shard_map/ppermute | solution.py:20
  26.1 39.9 %collective-permute-start.2 = (bf16[3,1,32,67,128]{4,2,3,1,0:T(8,128)(2,1)}, bf16[3,1,32,67,128]{4,2,3,1,0:T(8,128)(2,1)}, u32[]{:S(2)}, u32[]{:S(2)}) collective-permute-start(bf16[3,1,32,67,128]{4,2,3,1,0:T(8,128)(2,1)} %copy.34), channel_id=1, source_target_pairs={{0,1},{1,2},{2,3},{3,4},{4,5},{5,6},{6,7},{7,8},{8,9},{9,10},{10,1... | collective-permute-start | bytes 4939784 | tf_op jit(solution)/shard_map/ppermute | solution.py:17
  30.0 38.1 %collective-permute-start.3 = (bf16[3,1,32,67,128]{4,2,3,1,0:T(8,128)(2,1)}, bf16[3,1,32,67,128]{4,2,3,1,0:T(8,128)(2,1)}, u32[]{:S(2)}, u32[]{:S(2)}) collective-permute-start(bf16[3,1,32,67,128]{4,2,3,1,0:T(8,128)(2,1)} %copy.34), channel_id=1, source_target_pairs={{1,0},{2,1},{3,2},{4,3},{5,4},{6,5},{7,6},{8,7},{9,8},{10,9},{11,1... | collective-permute-start | bytes 4939784 | tf_op jit(solution)/shard_map/ppermute | solution.py:20
  78.5 85.6 %copy-start.1 = (bf16[8,16,2048]{2,1,0:T(8,128)(2,1)S(1)}, bf16[8,16,2048]{2,1,0:T(8,128)(2,1)}, u32[]{:S(2)}) copy-start(bf16[8,16,2048]{2,1,0:T(8,128)(2,1)} %param.9) | copy-start | bytes 1572868
  161.9 13.7 %collective-permute-start.4 = (bf16[1,8,4096]{2,1,0:T(8,128)(2,1)}, bf16[1,8,4096]{2,1,0:T(8,128)(2,1)}, u32[]{:S(2)}, u32[]{:S(2)}) collective-permute-start(bf16[1,8,4096]{2,1,0:T(8,128)(2,1)} %slice.48), channel_id=1, source_target_pairs={{32,0},{64,32},{96,64},{128,96},{160,128},{192,160},{224,192},{256... | collective-permute-start | bytes 196616 | tf_op jit(solution)/shard_map/ppermute | solution.py:28
  176.5 9.4 %collective-permute-start.5 = (bf16[5,1,4096]{2,1,0:T(2,128)(2,1)S(1)}, bf16[5,1,4096]{2,1,0:T(2,128)(2,1)S(1)}, u32[]{:S(2)}, u32[]{:S(2)}) collective-permute-start(bf16[5,1,4096]{2,1,0:T(2,128)(2,1)S(1)} %pad_maximum_fusion.4), channel_id=1, source_target_pairs={{0,31},{1,0},{2,1},{3,2},{4,3},{5,4},{6,5},{7,6},{8,7},{9,8},{10,9... | collective-permute-start | bytes 122888 | tf_op jit(solution)/shard_map/ppermute | solution.py:34
where the time goes:
time: 196 us; the launch traced here: 195 us
  local copies, waits for them, and re-layouts  60.9 us (31%)
  waiting for transfers between devices  42.9 us (22%)
  matrix products  40 us (20%)
  starting transfers between devices  36.1 us (18%)
  other arithmetic  10.3 us (5%)
  loops' own time  3.75 us (2%)
    ppermute x2, waiting for transfers between devices, padded(): lax.ppermute(lax.slice_in_dim(block, block.shape[dim] - width, None, axis...  24.8 us
    ppermute x2, starting transfers between devices, padded(): lax.ppermute(lax.slice_in_dim(block, 0, width, axis=dim), axis, backward)  17.5 us
    gather x4, local copies, waits for them, and re-layouts, coarse_row(): chosen = flat_blocks[listed]  12.7 us
    dot_general x24, matrix products, newton_schulz(): jnp.einsum('pij,pjk->pik', inverse, current, precision=lax.Precision.HIGH...  9.57 us
    ppermute x1, waiting for transfers between devices, from_behind(): return lax.ppermute(block, axis, route)  9.34 us
    dot_general x24, matrix products, newton_schulz(): jnp.einsum('pij,pjk->pik', middle, inverse, precision=lax.Precision.HIGHEST)  9.21 us
    ppermute x2, starting transfers between devices, padded(): lax.ppermute(lax.slice_in_dim(block, block.shape[dim] - width, None, axis...  8.43 us
    dot_general x20, matrix products, newton_schulz(): jnp.einsum('pij,pjk->pik', current, middle, precision=lax.Precision.HIGHEST)  7.98 us
  transfers between devices with their start and end apart: 6, of which 5 were waited for; matrix products, arithmetic and copies ran while one was open for 2% of the time, Pallas kernels for 0%

commit v1 on v0

v1 whole, which is shorter than its diff:
```python
import functools

import jax
import jax.numpy as jnp
from jax import lax
from jax.experimental import pallas as pl
from jax.experimental.pallas import tpu as pltpu
from jax.sharding import PartitionSpec as P

F32 = jnp.float32
BF16 = jnp.bfloat16
MESH = pl.DeviceIdType.MESH
NSI = 6
LOC = 12
K = 64
OB = 128
CLAT = 8
CLON = 16
NBLK = 32
NNB = 12
LEV = 32
NT = 33
PAD = 33
CHUNKS = ((0, 11), (11, 22), (22, 33))


def dot(a, b):
    return jnp.dot(a, b, preferred_element_type=F32)


def split(x):
    hi = x.astype(BF16)
    return hi, (x - hi.astype(F32)).astype(BF16)


def diagonal(x, left, right):
    first, second = x[:, :128], x[:, 128:]
    zero = jnp.zeros_like(first)
    return jnp.concatenate(
        [
            jnp.concatenate([first * left, zero], 1),
            jnp.concatenate([first * right, zero], 1),
            jnp.concatenate([zero, second * left], 1),
            jnp.concatenate([zero, second * right], 1),
        ],
        0,
    )


def kernel(
    na, nb, ens, w, bcol, innov, prec, cnt, nbs, out,
    sa, sg, sp, gall, nbp, msend, mrecv, ssend, srecv, own, s2, yz, zf, tb, csend, rrow, rcol, rcor, dd, xa, sx, so,
    scales, g_send, g_recv, n_send, n_recv, m_send, m_recv, s_send, s_recv, t_send, t_recv,
):
    ia, jb = lax.axis_index("lat"), lax.axis_index("lon")
    up, down = lax.rem(ia + na - 1, na), lax.rem(ia + 1, na)
    west, east = lax.rem(jb + nb - 1, nb), lax.rem(jb + 1, nb)

    barrier = pltpu.get_barrier_semaphore()
    for peer in ((up, jb), (down, jb), (ia, west), (ia, east), (up, west), (down, east)):
        pl.semaphore_signal(barrier, inc=1, device_id=peer, device_id_type=MESH)

    def remote(src, dst, send, recv, peer):
        return pltpu.make_async_remote_copy(
            src_ref=src, dst_ref=dst, send_sem=send, recv_sem=recv, device_id=peer, device_id_type=MESH
        )

    lane1 = lax.broadcasted_iota(jnp.int32, (1, 128), 1)
    left_f = (lane1 < 64).astype(F32)
    left, right = left_f.astype(BF16), (1.0 - left_f).astype(BF16)
    row128 = lax.broadcasted_iota(jnp.int32, (128, 128), 0)
    lane128 = lax.broadcasted_iota(jnp.int32, (128, 128), 1)
    averager = jnp.where(row128 // 64 == lane128 // 64, 1.0 / K, 0.0).astype(BF16)

    code = jnp.zeros((1, 128), jnp.int32)
    columns = jnp.concatenate([bcol[...], jnp.zeros((1, 128 - NBLK), jnp.int32)], 1)
    live = (lane1 < cnt[0, 0]) & (lane1 < NBLK)
    code = jnp.where(live, columns + 1, 0)
    msend[0] = jnp.broadcast_to(code, (8, 128))
    msend[1] = jnp.broadcast_to(pltpu.roll(code, 2 * NBLK, 1), (8, 128))
    code_own = pltpu.roll(code, NBLK, 1)
    nbp[1, :, 0:NNB] = nbs[...]

    chosen = jnp.where(row128 == jnp.broadcast_to(columns, (128, 128)), 1.0, 0.0)
    chosen = jnp.where(lane128 < NBLK, chosen, 0.0)
    chosen = jnp.transpose(chosen)[:NBLK].astype(BF16)
    state = ens[...].reshape(CLAT * CLON, LEV * K)
    picked = dot(chosen, state)
    stacked = jnp.concatenate([picked[:, 128 * t : 128 * (t + 1)] for t in range(16)], 0)
    anomaly = stacked - dot(stacked.astype(BF16), averager)
    for t in range(16):
        part = anomaly[NBLK * t : NBLK * (t + 1)]
        sa[pl.ds(2 * t * PAD, NBLK), :] = part
        sa[pl.ds((2 * t + 1) * PAD, NBLK), :] = pltpu.roll(part, 64, 1)
    sp[0] = jnp.sqrt(prec[...].astype(F32))
    sp[1] = innov[...].astype(F32) * sp[0]

    def blocks(step, carry):
        for i in range(16):
            b = step * 16 + i
            x = sa[pl.ds(b, LEV, stride=PAD), :][:, :K].astype(BF16)
            y = lax.dot_general(x, w[b], (((0,), (0,)), ((), ())), preferred_element_type=F32)
            root = sp[0, pl.ds(b, 1), :]
            ys = (y * root).astype(BF16)
            forced = sp[1, pl.ds(b, 1), :]
            tail = jnp.where(lax.broadcasted_iota(jnp.int32, (16, 128), 0) == 0, forced, 0.0).astype(BF16)
            g = lax.dot_general(
                jnp.concatenate([ys, tail], 0), ys, (((1,), (1,)), ((), ())), preferred_element_type=F32
            )
            sg[pl.ds(b, 72, stride=PAD), 0:K] = g[:72]
        return carry

    lax.fori_loop(0, 2, blocks, 0)

    wide = lax.broadcasted_iota(jnp.int32, (NBLK, 128), 1)
    zeros64 = jnp.zeros((NBLK, K), F32)

    def unit(k):
        return sg[pl.ds(k * PAD, NBLK), 0:K]

    for j in range(32):
        gall[1, j] = jnp.concatenate([unit(j), unit(j + 32)], 1).astype(BF16)
    gall[1, 32] = jnp.concatenate([unit(64), zeros64], 1).astype(BF16)

    pl.semaphore_wait(barrier, 6)
    first = [
        remote(gall.at[1], gall.at[0], g_send.at[0], g_recv.at[0], (ia, east)),
        remote(gall.at[1], gall.at[2], g_send.at[1], g_recv.at[1], (ia, west)),
        remote(nbp.at[1], nbp.at[0], n_send.at[0], n_recv.at[0], (up, jb)),
        remote(nbp.at[1], nbp.at[2], n_send.at[1], n_recv.at[1], (down, jb)),
        remote(msend.at[0], mrecv.at[0], m_send.at[0], m_recv.at[0], (ia, east)),
        remote(msend.at[1], mrecv.at[1], m_send.at[1], m_recv.at[1], (ia, west)),
    ]
    for copy in (first[4], first[5], first[2], first[3], first[0], first[1]):
        copy.start()

    def columns_of(r, carry):
        x = jnp.concatenate([ens[r, :, 128 * t : 128 * (t + 1)] for t in range(16)], 0)
        spread = (x.astype(F32) - dot(x, averager)).astype(BF16).astype(F32)
        for t in range(16):
            sx[r, pl.ds(t * 17, CLON), :] = spread[CLON * t : CLON * (t + 1)]
        for c in range(CLON):
            xa[r * CLON + c] = sx[r, pl.ds(c, 16, stride=17), :].astype(BF16)
        return carry

    lax.fori_loop(0, CLAT, columns_of, 0)

    for copy in first[2:]:
        copy.wait()
    code3 = mrecv[0, 0:1, :] + code_own + mrecv[1, 0:1, :]
    is_live = (code3 > 0).astype(F32)
    place = jnp.maximum(code3 - 1, 0)
    b_row = (place // CLON).astype(F32)
    b_col = (place % CLON + (lane1 // NBLK - 1) * CLON).astype(F32)
    point = lax.broadcasted_iota(jnp.int32, (32, 128), 0)
    p_row = (2 * (point // 8)).astype(F32)
    p_col = (2 * (point % 8)).astype(F32)
    weights = []
    for u in (-1, 0, 1):
        listed = nbp[u + 1]
        count = jnp.zeros((32, 128), F32)
        for n in range(NNB):
            count += (listed[:, n : n + 1] - 96 * (u + 1) == wide).astype(F32)
        dlat = (b_row + float(u * CLAT)) - p_row
        dlon = b_col - p_col
        taper = jnp.exp(-(dlat * dlat + dlon * dlon) / (2.0 * LOC * LOC))
        valid = ((ia - u >= 0) & (ia - u < na)).astype(F32)
        weights.append(jnp.where(wide < 96, count * taper * is_live * valid, 0.0))
    whi, wlo = split(jnp.concatenate(weights, 0))
    lhs = jnp.concatenate([whi, wlo], 0)[:, :96]

    first[0].wait()
    first[1].wait()
    second = []
    for n, (lo, hi) in enumerate(CHUNKS):
        for t in range(lo, hi):
            rhs = jnp.concatenate([gall[0, t], gall[1, t], gall[2, t]], 0)
            o = dot(lhs, rhs)
            o = o[:96] + o[96:]
            ssend[0, t] = o[:32].astype(BF16)
            own[t] = o[32:64]
            ssend[1, t] = o[64:].astype(BF16)
        span = pl.ds(lo, hi - lo)
        pair = [
            remote(ssend.at[0, span], srecv.at[0, span], s_send.at[0, n], s_recv.at[0, n], (down, jb)),
            remote(ssend.at[1, span], srecv.at[1, span], s_send.at[1, n], s_recv.at[1, n], (up, jb)),
        ]
        for copy in pair:
            copy.start()
        second.append(pair)
    for n, (lo, hi) in enumerate(CHUNKS):
        for copy in second[n]:
            copy.wait()
        for t in range(lo, hi):
            s2[pl.ds(t * PAD, 32), :] = own[t] + srecv[0, t].astype(F32) + srecv[1, t].astype(F32)

    row64 = lax.broadcasted_iota(jnp.int32, (K, 256), 0)
    lane256 = lax.broadcasted_iota(jnp.int32, (K, 256), 1)
    eye = (lane256 % 64 == row64).astype(F32)
    ones = jnp.where(
        lax.broadcasted_iota(jnp.int32, (256, 256), 0) // 64 == lax.broadcasted_iota(jnp.int32, (256, 256), 1) // 64,
        1.0, 0.0,
    ).astype(BF16)
    half = lax.broadcasted_iota(jnp.int32, (32, 128), 1) < 64
    half1 = lane1 < 64
    row16 = lax.broadcasted_iota(jnp.int32, (16, 256), 0)

    def two_rows(x):
        hi = x.astype(BF16).astype(F32)
        return jnp.where(row16 == 0, hi, jnp.where(row16 == 1, x - hi, 0.0)).astype(BF16)

    def product(a_hi, a_lo, b):
        b_hi, b_lo = split(b)
        o = dot(jnp.concatenate([a_hi, a_lo], 0), diagonal(b_hi, left, right))
        return o[:K] + o[K:] + dot(a_hi, diagonal(b_lo, left, right))

    def keep(g, y, z):
        y_hi, y_lo = split(y)
        z_hi, z_lo = split(z)
        yz[g, 0:64] = y_hi
        yz[g, 64:128] = z_hi
        yz[g, 128:192] = y_lo
        yz[g, 192:256] = z_lo

    for g in range(8):
        parts, proj = [], []
        for m in (2 * g, 2 * g + 1):
            x0 = s2[pl.ds(2 * m, 32, stride=PAD), :]
            x1 = s2[pl.ds(2 * m + 1, 32, stride=PAD), :]
            parts.append(
                jnp.concatenate(
                    [jnp.where(half, x0, pltpu.roll(x1, 64, 1)), jnp.where(half, pltpu.roll(x0, 64, 1), x1)], 0
                )
            )
            q0 = s2[pl.ds(32 * PAD + 2 * m, 1), :]
            q1 = s2[pl.ds(32 * PAD + 2 * m + 1, 1), :]
            proj.append(jnp.where(half1, q0, pltpu.roll(q1, 64, 1)))
        gram = jnp.concatenate(parts, 1) + (K - 1.0) * eye
        sums = dot(two_rows(jnp.sum(gram * gram, axis=0, keepdims=True)), ones)
        inv = 1.0 / jnp.sqrt(sums[0:1] + sums[1:2])
        scales[g, 0:1] = inv
        scales[g, 1:2] = jnp.concatenate(proj, 1)
        x = gram * inv
        middle = 1.5 * eye - 0.5 * x
        x_hi, x_lo = split(x)
        keep(g, product(x_hi, x_lo, middle), middle)

    def middle_of(g):
        z_hi, z_lo = yz[g, 64:128], yz[g, 192:256]
        o = dot(jnp.concatenate([z_hi, z_lo], 0), diagonal(yz[g, 0:64], left, right))
        o = o[:K] + o[K:] + dot(z_hi, diagonal(yz[g, 128:192], left, right))
        return 1.5 * eye - 0.5 * o

    def turn(step, carry):
        for g in range(8):
            zf[g] = middle_of(g)
        for g in range(8):
            m_hi, m_lo = split(zf[g])
            o = dot(yz[g], diagonal(m_hi, left, right))
            e = dot(yz[g, 0:128], diagonal(m_lo, left, right))
            keep(g, o[0:64] + o[128:192] + e[0:64], o[64:128] + o[192:256] + e[64:128])
        return carry

    lax.fori_loop(0, NSI - 2, turn, 0)
    for g in range(8):
        zf[g] = product(yz[g, 64:128], yz[g, 192:256], middle_of(g))
    for g in range(8):
        z = zf[g]
        z_hi, z_lo = split(z)
        inv = scales[g, 0:1]
        o = dot(two_rows(scales[g, 1:2]), diagonal(z_hi, left, right))
        e = dot(two_rows(scales[g, 1:2]), diagonal(z_lo, left, right))
        h = o[0:1] + o[1:2] + e[0:1]
        d_hi, d_lo = split(z * h)
        s = dot(jnp.concatenate([d_hi, d_lo], 0), ones)
        t = z * (jnp.sqrt(K - 1.0) * jnp.sqrt(inv)) + (s[:K] + s[K:]) * inv
        tb[2 * g] = t[:, :128].astype(BF16)
        tb[2 * g + 1] = t[:, 128:].astype(BF16)

    half64 = lax.broadcasted_iota(jnp.int32, (K, 128), 1) < 64
    for i in range(2):
        p0 = tb[8 * i].astype(F32)
        p1 = tb[8 * i + 4].astype(F32)
        csend[i] = jnp.where(half64, p0, pltpu.roll(p1, 64, 1)).astype(BF16)
    third = [
        remote(tb.at[pl.ds(0, 4)], rrow, t_send.at[0], t_recv.at[0], (up, jb)),
        remote(csend, rcol, t_send.at[1], t_recv.at[1], (ia, west)),
        remote(csend.at[0], rcor, t_send.at[2], t_recv.at[2], (up, west)),
    ]
    for copy in third:
        copy.start()

    zero64 = jnp.zeros((K, 128), F32)

    def expand(pair):
        v = pair.astype(F32)
        r = pltpu.roll(v, 64, 1)
        d0 = jnp.concatenate([jnp.where(half64, v, zero64), jnp.where(half64, zero64, r)], 0)
        d1 = jnp.concatenate([jnp.where(half64, r, zero64), jnp.where(half64, zero64, v)], 0)
        return d0.astype(BF16), d1.astype(BF16)

    for m in range(16):
        a, c = m // 4, 2 * (m % 4)
        dd[a, c], dd[a, c + 1] = expand(tb[m])

    last = ia == na - 1
    for copy in third:
        copy.wait()
    edge = last.astype(F32)
    for i in range(4):
        mixed = rrow[i].astype(F32) * (1.0 - edge) + tb[12 + i].astype(F32) * edge
        dd[4, 2 * i], dd[4, 2 * i + 1] = expand(mixed)
    for i in range(2):
        dd[2 * i, 8], dd[2 * i + 1, 8] = expand(rcol[i])
    bottom = pltpu.roll(rcol[1].astype(F32), 64, 1)
    dd[4, 8] = expand(rcor[...].astype(F32) * (1.0 - edge) + bottom * edge)[0]

    def finish(a, carry):
        none = jnp.zeros((16, 128), BF16)
        for c in range(8):
            base = 2 * a * CLON + 2 * c
            ee, eo = xa[base], xa[base + 1] * 0.5
            oe, oo = xa[base + CLON] * 0.5, xa[base + CLON + 1] * 0.25
            lower = jnp.concatenate([jnp.concatenate([oe, none], 1), jnp.concatenate([oo, oo], 1)], 0)
            upper = jnp.concatenate([jnp.concatenate([ee, none], 1), jnp.concatenate([eo, eo], 1), lower], 0)
            o = dot(upper, dd[a, c : c + 2].reshape(256, 128))
            e = dot(lower, dd[a + 1, c : c + 2].reshape(256, 128))
            so[0, pl.ds(2 * c, 16, stride=17), :] = o[0:16]
            so[0, pl.ds(2 * c + 1, 16, stride=17), :] = o[16:32]
            so[1, pl.ds(2 * c, 16, stride=17), :] = o[32:48] + e[0:16]
            so[1, pl.ds(2 * c + 1, 16, stride=17), :] = o[48:64] + e[16:32]
        for i in range(2):
            r = 2 * a + i
            x = jnp.concatenate([ens[r, :, 128 * t : 128 * (t + 1)] for t in range(16)], 0)
            center = dot(x, averager)
            for t in range(16):
                rows = so[i, pl.ds(t * 17, CLON), :] + center[CLON * t : CLON * (t + 1)]
                out[r, :, 128 * t : 128 * (t + 1)] = rows.astype(BF16)
        return carry

    lax.fori_loop(0, 4, finish, 0)


def solution(mesh):
    na, nb = mesh.shape["lat"], mesh.shape["lon"]

    def body(ensemble, channel_weights, block_column, innovation, error_precision, block_count, neighbours):
        vmem = pl.BlockSpec(memory_space=pltpu.VMEM)
        smem = pl.BlockSpec(memory_space=pltpu.SMEM)
        dma = pltpu.SemaphoreType.DMA
        return pl.pallas_call(
            functools.partial(kernel, na, nb),
            out_shape=jax.ShapeDtypeStruct(ensemble.shape, BF16),
            in_specs=[vmem, vmem, vmem, vmem, vmem, smem, vmem],
            out_specs=vmem,
            scratch_shapes=[
                pltpu.VMEM((LEV * PAD, 128), F32),
                pltpu.VMEM((72 * PAD, 128), F32),
                pltpu.VMEM((2, NBLK, OB), F32),
                pltpu.VMEM((3, NT, NBLK, 128), BF16),
                pltpu.VMEM((3, 32, 128), jnp.int32),
                pltpu.VMEM((2, 8, 128), jnp.int32),
                pltpu.VMEM((2, 8, 128), jnp.int32),
                pltpu.VMEM((2, NT, 32, 128), BF16),
                pltpu.VMEM((2, NT, 32, 128), BF16),
                pltpu.VMEM((NT, 32, 128), F32),
                pltpu.VMEM((NT * PAD, 128), F32),
                pltpu.VMEM((8, 256, 256), BF16),
                pltpu.VMEM((8, K, 256), F32),
                pltpu.VMEM((16, K, 128), BF16),
                pltpu.VMEM((2, K, 128), BF16),
                pltpu.VMEM((4, K, 128), BF16),
                pltpu.VMEM((2, K, 128), BF16),
                pltpu.VMEM((K, 128), BF16),
                pltpu.VMEM((5, 9, 128, 128), BF16),
                pltpu.VMEM((CLAT * CLON, 16, 128), BF16),
                pltpu.VMEM((CLAT, 272, 128), F32),
                pltpu.VMEM((2, 272, 128), F32),
                pltpu.VMEM((8, 8, 256), F32),
                dma((2,)), dma((2,)), dma((2,)), dma((2,)), dma((2,)), dma((2,)),
                dma((2, 3)), dma((2, 3)), dma((3,)), dma((3,)),
            ],
            compiler_params=pltpu.CompilerParams(
                collective_id=0, has_side_effects=True, vmem_limit_bytes=48 * 2**20
            ),
        )(
            ensemble,
            channel_weights[0, 0],
            block_column[0],
            innovation[0, 0],
            error_precision[0, 0],
            block_count,
            neighbours.reshape(32, NNB),
        )

    return jax.shard_map(
        body,
        mesh=mesh,
        in_specs=(
            P("lat", "lon", None),
            P("lat", "lon", None, None, None),
            P("lat", "lon", None),
            P("lat", "lon", None, None),
            P("lat", "lon", None, None),
            P("lat", "lon"),
            P("lat", "lon", None),
        ),
        out_specs=P("lat", "lon", None),
        check_vma=False,
    )
```

time: 196 us -> 48.4 us (0.25)
  local copies, waits for them, and re-layouts: 60.9 us -> 4.85 us
  waiting for transfers between devices: 42.9 us -> 0 us
  Pallas kernels: 0 us -> 42.1 us
  matrix products: 40 us -> 0 us
  starting transfers between devices: 36.1 us -> 0 us
  other arithmetic: 10.3 us -> 0 us
  loops' own time: 3.75 us -> 0 us
    ppermute x6 -> x0, waiting for transfers between devices: 42.9 us -> none  [the longest x2 24.8 us: padded(): lax.ppermute(lax.slice_in_dim(block, block.shape[dim] - width, None, axis...]
    pallas_call x0 -> x1, Pallas kernels: none -> 42.1 us  [body(): pl.pallas_call(functools.partial(kernel, na, nb), out_shape=jax.ShapeDtyp...]
    dot_general x86 -> x0, matrix products: 40 us -> none  [the longest x24 9.57 us: newton_schulz(): jnp.einsum('pij,pjk->pik', inverse, current, precision=lax.Precision.HIGH...]
    ppermute x6 -> x0, starting transfers between devices: 36.1 us -> none  [the longest x2 17.5 us: padded(): lax.ppermute(lax.slice_in_dim(block, 0, width, axis=dim), axis, backward)]
    gather x33 -> x0, local copies, waits for them, and re-layouts: 34.7 us -> none  [the longest x4 12.7 us: coarse_row(): chosen = flat_blocks[listed]]
    slice x5 -> x0, local copies, waits for them, and re-layouts: 7.42 us -> none  [the longest x1 3.49 us: body(): flat_blocks = flat_packed[:, :members]]
    unnamed x9 -> x13, local copies, waits for them, and re-layouts: 0.05 us -> 4.85 us
    concatenate x11 -> x0, other arithmetic: 4.78 us -> none  [the longest x8 2.8 us: coarse_row(): root_weight = jnp.sqrt(taper[:, :, None] * flat_facts[listed, 1])]
  transfers between devices with their start and end apart: 6 -> 0, of which waited for: 5 -> 0; matrix products, arithmetic and copies ran while one was open for 2% -> 0% of each run, Pallas kernels for 0% -> 0%
where the time goes in v1:
time: 48.4 us; the launch traced here: 47.7 us
  Pallas kernels  42.1 us (87%)
  local copies, waits for them, and re-layouts  4.85 us (10%)
  between operations  0.69 us (1%)
    pallas_call x1, Pallas kernels, body(): pl.pallas_call(functools.partial(kernel, na, nb), out_shape=jax.ShapeDtyp...  42.1 us
    unnamed x13, local copies, waits for them, and re-layouts  4.85 us

profile of v1, /device:TPU:1, one launch (start us, length us, event | category | flops | bytes accessed | tf_op | source)
XLA Modules:
  0.0 47.7 jit_solution(7277381612937233967)
XLA Ops:
  0.0 0.0 copy-start.3
  0.7 0.0 copy-start.5
  0.7 0.0 copy-done.3
  0.7 0.6 %copy-done.5 = s32[1,1,32]{2,1,0:T(1,128)S(1)} copy-done((s32[1,1,32]{2,1,0:T(1,128)S(1)}, s32[1,1,32]{2,1,0:T(1,128)}, u32[]{:S(2)}) %copy-start.5) | copy-done | bytes 152
  1.3 0.0 copy-start
  1.3 1.0 %copy-done = bf16[8,16,2048]{2,1,0:T(8,128)(2,1)S(1)} copy-done((bf16[8,16,2048]{2,1,0:T(8,128)(2,1)S(1)}, bf16[8,16,2048]{2,1,0:T(8,128)(2,1)}, u32[]{:S(2)}) %copy-start) | copy-done | bytes 524312
  2.4 0.0 copy-start.1
  2.4 0.9 %copy-done.1 = bf16[1,1,32,32,128]{4,3,2,1,0:T(8,128)(2,1)S(1)} copy-done((bf16[1,1,32,32,128]{4,3,2,1,0:T(8,128)(2,1)S(1)}, bf16[1,1,32,32,128]{4,3,2,1,0:T(8,128)(2,1)}, u32[]{:S(2)}) %copy-start.1) | copy-done | bytes 262168
  3.3 0.0 copy-start.2
  3.3 0.7 %copy-done.2 = s32[4,8,12]{2,1,0:T(8,128)S(1)} copy-done((s32[4,8,12]{2,1,0:T(8,128)S(1)}, s32[4,8,12]{2,1,0:T(8,128)}, u32[]{:S(2)}) %copy-start.2) | copy-done | bytes 1560
  4.0 0.0 copy-start.4
  4.0 0.7 %copy-done.4 = bf16[1,1,32,128]{3,2,1,0:T(8,128)(2,1)S(1)} copy-done((bf16[1,1,32,128]{3,2,1,0:T(8,128)(2,1)S(1)}, bf16[1,1,32,128]{3,2,1,0:T(8,128)(2,1)}, u32[]{:S(2)}) %copy-start.4) | copy-done | bytes 8216
  4.7 42.1 %shard_map.73 = bf16[8,16,2048]{2,1,0:T(8,128)(2,1)S(1)} custom-call(bf16[8,16,2048]{2,1,0:T(8,128)(2,1)S(1)} %copy-done, bf16[32,32,128]{2,1,0:T(8,128)(2,1)S(1)} %bitcast.5, s32[1,32]{1,0:T(1,128)S(1)} %bitcast.9, bf16[32,128]{1,0:T(8,128)(2,1)S(1)} %bitcast.7, bf16[32,128]{1,0:T(8,128)(2,1)S(1)} %bitcast.8, s32[1,1]{1,0:T(1,128)S(6)} %copy.9.cnt, ...), custom_call_target="tpu_custom_call" | custom-call | tf_op jit(solution)/shard_map/pallas_call | solution.py:351
  46.9 0.8 %copy.10 = bf16[8,16,2048]{2,1,0:T(8,128)(2,1)} copy(bf16[8,16,2048]{2,1,0:T(8,128)(2,1)S(1)} %shard_map.73) | data formatting | bytes 1048576
Async XLA Ops:
  0.0 0.7 %copy-start.3 = (bf16[1,1,32,128]{3,2,1,0:T(8,128)(2,1)S(1)}, bf16[1,1,32,128]{3,2,1,0:T(8,128)(2,1)}, u32[]{:S(2)}) copy-start(bf16[1,1,32,128]{3,2,1,0:T(8,128)(2,1)} %param.10) | copy-start | bytes 24580
  0.7 0.7 %copy-start.5 = (s32[1,1,32]{2,1,0:T(1,128)S(1)}, s32[1,1,32]{2,1,0:T(1,128)}, u32[]{:S(2)}) copy-start(s32[1,1,32]{2,1,0:T(1,128)} %param.9) | copy-start | bytes 388
  1.3 1.0 %copy-start = (bf16[8,16,2048]{2,1,0:T(8,128)(2,1)S(1)}, bf16[8,16,2048]{2,1,0:T(8,128)(2,1)}, u32[]{:S(2)}) copy-start(bf16[8,16,2048]{2,1,0:T(8,128)(2,1)} %ens.1) | copy-start | bytes 1572868
  2.4 0.9 %copy-start.1 = (bf16[1,1,32,32,128]{4,3,2,1,0:T(8,128)(2,1)S(1)}, bf16[1,1,32,32,128]{4,3,2,1,0:T(8,128)(2,1)}, u32[]{:S(2)}) copy-start(bf16[1,1,32,32,128]{4,3,2,1,0:T(8,128)(2,1)} %param.8) | copy-start | bytes 786436
  3.3 0.7 %copy-start.2 = (s32[4,8,12]{2,1,0:T(8,128)S(1)}, s32[4,8,12]{2,1,0:T(8,128)}, u32[]{:S(2)}) copy-start(s32[4,8,12]{2,1,0:T(8,128)} %param.13) | copy-start | bytes 4612
  4.0 0.7 %copy-start.4 = (bf16[1,1,32,128]{3,2,1,0:T(8,128)(2,1)S(1)}, bf16[1,1,32,128]{3,2,1,0:T(8,128)(2,1)}, u32[]{:S(2)}) copy-start(bf16[1,1,32,128]{3,2,1,0:T(8,128)(2,1)} %param.11) | copy-start | bytes 24580

commit v2 on v1

--- a/solution.py
+++ b/solution.py
@@ -19,9 +19,10 @@
 NBLK = 32
 NNB = 12
 LEV = 32
-NT = 33
+NT = 17
 PAD = 33
-CHUNKS = ((0, 11), (11, 22), (22, 33))
+CHUNKS = ((0, 4), (4, 8), (8, 12), (12, 17))
+ORDER = (0, 1, 2, 3, 4, 5, 6, 7, 8, 16, 24, 9, 10, 11, 12, 13, 14, 15) + tuple(range(17, 24)) + tuple(range(25, 32))
 
 
 def dot(a, b):
@@ -48,10 +49,18 @@
 
 
 def kernel(
-    na, nb, ens, w, bcol, innov, prec, cnt, nbs, out,
-    sa, sg, sp, gall, nbp, msend, mrecv, ssend, srecv, own, s2, yz, zf, tb, csend, rrow, rcol, rcor, dd, xa, sx, so,
+    na, nb, ens_h, w_h, bcol_h, innov_h, prec_h, cnt_h, nbs_h, out,
+    ens, w, bcol, innov, prec, cnt, nbs, in_sem, yb, sa, sg, sp, gall, nbp, msend, mrecv, ssend, srecv, own, s2, yz, zf, tb, csend, rrow, rcol, rcor, dd, xa, sx, so,
     scales, g_send, g_recv, n_send, n_recv, m_send, m_recv, s_send, s_recv, t_send, t_recv,
 ):
+    loads = [
+        pltpu.make_async_copy(src, dst, in_sem.at[i])
+        for i, (src, dst) in enumerate(
+            ((bcol_h, bcol), (cnt_h, cnt), (ens_h, ens), (w_h, w), (prec_h, prec), (innov_h, innov), (nbs_h, nbs))
+        )
+    ]
+    for load in loads:
+        load.start()
     ia, jb = lax.axis_index("lat"), lax.axis_index("lon")
     up, down = lax.rem(ia + na - 1, na), lax.rem(ia + 1, na)
     west, east = lax.rem(jb + nb - 1, nb), lax.rem(jb + 1, nb)
@@ -71,6 +80,9 @@
     row128 = lax.broadcasted_iota(jnp.int32, (128, 128), 0)
     lane128 = lax.broadcasted_iota(jnp.int32, (128, 128), 1)
     averager = jnp.where(row128 // 64 == lane128 // 64, 1.0 / K, 0.0).astype(BF16)
+
+    for load in loads:
+        load.wait()
 
     code = jnp.zeros((1, 128), jnp.int32)
     columns = jnp.concatenate([bcol[...], jnp.zeros((1, 128 - NBLK), jnp.int32)], 1)
@@ -79,7 +91,8 @@
     msend[0] = jnp.broadcast_to(code, (8, 128))
     msend[1] = jnp.broadcast_to(pltpu.roll(code, 2 * NBLK, 1), (8, 128))
     code_own = pltpu.roll(code, NBLK, 1)
-    nbp[1, :, 0:NNB] = nbs[...]
+    for to, start, rows in ((0, 0, 8), (8, 8, 1), (9, 16, 1), (10, 24, 1), (11, 9, 7), (18, 17, 7), (25, 25, 7)):
+        nbp[1, to : to + rows, 0:NNB] = nbs[start : start + rows]
 
     chosen = jnp.where(row128 == jnp.broadcast_to(columns, (128, 128)), 1.0, 0.0)
     chosen = jnp.where(lane128 < NBLK, chosen, 0.0)
@@ -95,43 +108,59 @@
     sp[0] = jnp.sqrt(prec[...].astype(F32))
     sp[1] = innov[...].astype(F32) * sp[0]
 
-    def blocks(step, carry):
-        for i in range(16):
-            b = step * 16 + i
+    U1, U2, REP = 32, 32, 1
+
+    def observed(step, carry):
+        for i in range(U1):
+            b = lax.rem(step, 32 // U1) * U1 + i
             x = sa[pl.ds(b, LEV, stride=PAD), :][:, :K].astype(BF16)
             y = lax.dot_general(x, w[b], (((0,), (0,)), ((), ())), preferred_element_type=F32)
-            root = sp[0, pl.ds(b, 1), :]
-            ys = (y * root).astype(BF16)
+            yb[b, 0:K] = (y * sp[0, pl.ds(b, 1), :]).astype(BF16)
             forced = sp[1, pl.ds(b, 1), :]
-            tail = jnp.where(lax.broadcasted_iota(jnp.int32, (16, 128), 0) == 0, forced, 0.0).astype(BF16)
-            g = lax.dot_general(
-                jnp.concatenate([ys, tail], 0), ys, (((1,), (1,)), ((), ())), preferred_element_type=F32
-            )
+            yb[b, K : K + 16] = jnp.where(lax.broadcasted_iota(jnp.int32, (16, 128), 0) == 0, forced, 0.0).astype(BF16)
+        return carry
+
+    def squared(step, carry):
+        for i in range(U2):
+            b = lax.rem(step, 32 // U2) * U2 + i
+            g = lax.dot_general(yb[b], yb[b, 0:K], (((1,), (1,)), ((), ())), preferred_element_type=F32)
             sg[pl.ds(b, 72, stride=PAD), 0:K] = g[:72]
         return carry
 
-    lax.fori_loop(0, 2, blocks, 0)
+    lax.fori_loop(0, 32 // U1 * REP, observed, 0)
+    lax.fori_loop(0, 32 // U2 * REP, squared, 0)
 
     wide = lax.broadcasted_iota(jnp.int32, (NBLK, 128), 1)
-    zeros64 = jnp.zeros((NBLK, K), F32)
-
     def unit(k):
-        return sg[pl.ds(k * PAD, NBLK), 0:K]
-
-    for j in range(32):
-        gall[1, j] = jnp.concatenate([unit(j), unit(j + 32)], 1).astype(BF16)
-    gall[1, 32] = jnp.concatenate([unit(64), zeros64], 1).astype(BF16)
+        return sg[pl.ds(k * PAD, NBLK), :]
+
+    for i in range(16):
+        k = i + 16
+        low = unit(i) if i == 0 else jnp.where(wide >= i, unit(i), pltpu.roll(unit(63 - i), 64 + i, 1))
+        high = jnp.where(wide >= 64 + k, pltpu.roll(unit(k), 64, 1), pltpu.roll(unit(63 - k), k, 1))
+        gall[1, i] = jnp.where(wide < 64, low, high).astype(BF16)
+    spine = jnp.zeros((NBLK, 128), F32)
+    for k in range(32, 64):
+        spine = jnp.where(wide == k, unit(k), spine)
+    gall[1, 16] = jnp.where(wide < 64, unit(64), pltpu.roll(spine, 64, 1)).astype(BF16)
 
     pl.semaphore_wait(barrier, 6)
-    first = [
-        remote(gall.at[1], gall.at[0], g_send.at[0], g_recv.at[0], (ia, east)),
-        remote(gall.at[1], gall.at[2], g_send.at[1], g_recv.at[1], (ia, west)),
+    facts = [
         remote(nbp.at[1], nbp.at[0], n_send.at[0], n_recv.at[0], (up, jb)),
         remote(nbp.at[1], nbp.at[2], n_send.at[1], n_recv.at[1], (down, jb)),
         remote(msend.at[0], mrecv.at[0], m_send.at[0], m_recv.at[0], (ia, east)),
         remote(msend.at[1], mrecv.at[1], m_send.at[1], m_recv.at[1], (ia, west)),
     ]
-    for copy in (first[4], first[5], first[2], first[3], first[0], first[1]):
+    first = []
+    for n, (lo, hi) in enumerate(CHUNKS):
+        span = pl.ds(lo, hi - lo)
+        first.append(
+            [
+                remote(gall.at[1, span], gall.at[0, span], g_send.at[0, n], g_recv.at[0, n], (ia, east)),
+                remote(gall.at[1, span], gall.at[2, span], g_send.at[1, n], g_recv.at[1, n], (ia, west)),
+            ]
+        )
+    for copy in facts + [copy for pair in first for copy in pair]:
         copy.start()
 
     def columns_of(r, carry):
@@ -145,7 +174,7 @@
 
     lax.fori_loop(0, CLAT, columns_of, 0)
 
-    for copy in first[2:]:
+    for copy in facts:
         copy.wait()
     code3 = mrecv[0, 0:1, :] + code_own + mrecv[1, 0:1, :]
     is_live = (code3 > 0).astype(F32)
@@ -153,6 +182,11 @@
     b_row = (place // CLON).astype(F32)
     b_col = (place % CLON + (lane1 // NBLK - 1) * CLON).astype(F32)
     point = lax.broadcasted_iota(jnp.int32, (32, 128), 0)
+    point = jnp.where(
+        point < 8,
+        point,
+        jnp.where(point < 11, 8 * (point - 7), jnp.where(point < 18, point - 2, jnp.where(point < 25, point - 1, point))),
+    )
     p_row = (2 * (point // 8)).astype(F32)
     p_col = (2 * (point % 8)).astype(F32)
     weights = []
@@ -169,17 +203,20 @@
     whi, wlo = split(jnp.concatenate(weights, 0))
     lhs = jnp.concatenate([whi, wlo], 0)[:, :96]
 
-    first[0].wait()
-    first[1].wait()
     second = []
     for n, (lo, hi) in enumerate(CHUNKS):
-        for t in range(lo, hi):
-            rhs = jnp.concatenate([gall[0, t], gall[1, t], gall[2, t]], 0)
+        for copy in first[n]:
+            copy.wait()
+        for t in range(lo, hi, 2):
+            ts = range(t, min(t + 2, hi))
+            rhs = jnp.concatenate([jnp.concatenate([gall[v, i] for i in ts], 1) for v in range(3)], 0)
             o = dot(lhs, rhs)
             o = o[:96] + o[96:]
-            ssend[0, t] = o[:32].astype(BF16)
-            own[t] = o[32:64]
-            ssend[1, t] = o[64:].astype(BF16)
+            for i in ts:
+                part = o[:, 128 * (i - t) : 128 * (i - t + 1)]
+                ssend[0, i] = part[:32].astype(BF16)
+                own[i] = part[32:64]
+                ssend[1, i] = part[64:].astype(BF16)
         span = pl.ds(lo, hi - lo)
         pair = [
             remote(ssend.at[0, span], srecv.at[0, span], s_send.at[0, n], s_recv.at[0, n], (down, jb)),
@@ -191,9 +228,17 @@
     for n, (lo, hi) in enumerate(CHUNKS):
         for copy in second[n]:
             copy.wait()
-        for t in range(lo, hi):
-            s2[pl.ds(t * PAD, 32), :] = own[t] + srecv[0, t].astype(F32) + srecv[1, t].astype(F32)
-
+        for i in range(lo, hi):
+            tile = own[i] + srecv[0, i].astype(F32) + srecv[1, i].astype(F32)
+            if i == 16:
+                s2[pl.ds(64 * PAD, 32), :] = tile
+                s2[pl.ds(65 * PAD, 32), :] = pltpu.roll(tile, 64, 1)
+                continue
+            k = i + 16
+            s2[pl.ds(i * PAD, 32), :] = tile
+            s2[pl.ds((63 - i) * PAD, 32), :] = pltpu.roll(tile, 64 - i, 1)
+            s2[pl.ds(k * PAD, 32), :] = pltpu.roll(tile, 64, 1)
+            s2[pl.ds((63 - k) * PAD, 32), :] = pltpu.roll(tile, 128 - k, 1)
     row64 = lax.broadcasted_iota(jnp.int32, (K, 256), 0)
     lane256 = lax.broadcasted_iota(jnp.int32, (K, 256), 1)
     eye = (lane256 % 64 == row64).astype(F32)
@@ -201,7 +246,12 @@
         lax.broadcasted_iota(jnp.int32, (256, 256), 0) // 64 == lax.broadcasted_iota(jnp.int32, (256, 256), 1) // 64,
         1.0, 0.0,
     ).astype(BF16)
-    half = lax.broadcasted_iota(jnp.int32, (32, 128), 1) < 64
+    half64 = lax.broadcasted_iota(jnp.int32, (K, 128), 1) < 64
+    row_k = lax.broadcasted_iota(jnp.int32, (K, 128), 0)
+    lane_k = lax.broadcasted_iota(jnp.int32, (K, 128), 1)
+    above = (lane_k > row_k) & (lane_k < 64)
+    first_diagonal = (lane_k == row_k) & (row_k < 32)
+    last_diagonal = (lane_k == row_k) & (row_k >= 32)
     half1 = lane1 < 64
     row16 = lax.broadcasted_iota(jnp.int32, (16, 256), 0)
 
@@ -222,25 +272,35 @@
         yz[g, 128:192] = y_lo
         yz[g, 192:256] = z_lo
 
-    for g in range(8):
+    def symmetric(m):
+        upper, own_diagonal = [], []
+        for p in (2 * m, 2 * m + 1):
+            v = s2[pl.ds(p, K, stride=PAD), :]
+            d = jnp.broadcast_to(s2[pl.ds(65 * PAD + p, 1), :], (K, 128))
+            upper.append(jnp.where(above, v, 0.0))
+            own_diagonal.append(jnp.where(first_diagonal, v, jnp.where(last_diagonal, d, 0.0)))
+        whole = jnp.transpose(jnp.concatenate(upper, 0))[:K]
+        second_half = pltpu.roll(upper[1] + own_diagonal[1], 64, 1)
+        return whole + jnp.where(half64, upper[0] + own_diagonal[0], second_half)
+
+    def begin(g):
         parts, proj = [], []
         for m in (2 * g, 2 * g + 1):
-            x0 = s2[pl.ds(2 * m, 32, stride=PAD), :]
-            x1 = s2[pl.ds(2 * m + 1, 32, stride=PAD), :]
-            parts.append(
-                jnp.concatenate(
-                    [jnp.where(half, x0, pltpu.roll(x1, 64, 1)), jnp.where(half, pltpu.roll(x0, 64, 1), x1)], 0
-                )
-            )
-            q0 = s2[pl.ds(32 * PAD + 2 * m, 1), :]
-            q1 = s2[pl.ds(32 * PAD + 2 * m + 1, 1), :]
+            parts.append(symmetric(m))
+            q0 = s2[pl.ds(64 * PAD + 2 * m, 1), :]
+            q1 = s2[pl.ds(64 * PAD + 2 * m + 1, 1), :]
             proj.append(jnp.where(half1, q0, pltpu.roll(q1, 64, 1)))
         gram = jnp.concatenate(parts, 1) + (K - 1.0) * eye
-        sums = dot(two_rows(jnp.sum(gram * gram, axis=0, keepdims=True)), ones)
-        inv = 1.0 / jnp.sqrt(sums[0:1] + sums[1:2])
-        scales[g, 0:1] = inv
+        zf[g] = gram
         scales[g, 1:2] = jnp.concatenate(proj, 1)
-        x = gram * inv
+        scales[g, 0:1] = jnp.sum(gram * gram, axis=0, keepdims=True)
+
+    def scale(g):
+        sums = dot(two_rows(scales[g, 0:1]), ones)
+        scales[g, 0:1] = 1.0 / jnp.sqrt(sums[0:1] + sums[1:2])
+
+    def first_step(g):
+        x = zf[g] * scales[g, 0:1]
         middle = 1.5 * eye - 0.5 * x
         x_hi, x_lo = split(x)
         keep(g, product(x_hi, x_lo, middle), middle)
@@ -251,37 +311,74 @@
         o = o[:K] + o[K:] + dot(z_hi, diagonal(yz[g, 128:192], left, right))
         return 1.5 * eye - 0.5 * o
 
-    def turn(step, carry):
-        for g in range(8):
-            zf[g] = middle_of(g)
-        for g in range(8):
-            m_hi, m_lo = split(zf[g])
-            o = dot(yz[g], diagonal(m_hi, left, right))
-            e = dot(yz[g, 0:128], diagonal(m_lo, left, right))
-            keep(g, o[0:64] + o[128:192] + e[0:64], o[64:128] + o[192:256] + e[64:128])
-        return carry
-
-    lax.fori_loop(0, NSI - 2, turn, 0)
-    for g in range(8):
-        zf[g] = product(yz[g, 64:128], yz[g, 192:256], middle_of(g))
-    for g in range(8):
-        z = zf[g]
-        z_hi, z_lo = split(z)
-        inv = scales[g, 0:1]
-        o = dot(two_rows(scales[g, 1:2]), diagonal(z_hi, left, right))
-        e = dot(two_rows(scales[g, 1:2]), diagonal(z_lo, left, right))
-        h = o[0:1] + o[1:2] + e[0:1]
-        d_hi, d_lo = split(z * h)
-        s = dot(jnp.concatenate([d_hi, d_lo], 0), ones)
-        t = z * (jnp.sqrt(K - 1.0) * jnp.sqrt(inv)) + (s[:K] + s[K:]) * inv
-        tb[2 * g] = t[:, :128].astype(BF16)
-        tb[2 * g + 1] = t[:, 128:].astype(BF16)
-
-    half64 = lax.broadcasted_iota(jnp.int32, (K, 128), 1) < 64
-    for i in range(2):
-        p0 = tb[8 * i].astype(F32)
-        p1 = tb[8 * i + 4].astype(F32)
-        csend[i] = jnp.where(half64, p0, pltpu.roll(p1, 64, 1)).astype(BF16)
+    SEP = 1
+    def apart(f):
+        if SEP:
+            pl.when(ia >= 0)(f)
+        else:
+            f()
+
+    def invert(groups):
+        def opening():
+            for g in groups:
+                begin(g)
+        apart(opening)
+        def scaling():
+            for g in groups:
+                scale(g)
+        apart(scaling)
+        def start():
+            for g in groups:
+                first_step(g)
+        apart(start)
+
+        def turn(step, carry):
+            def one():
+                for g in groups:
+                    zf[g] = middle_of(g)
+            apart(one)
+            def two():
+                for g in groups:
+                    m_hi, m_lo = split(zf[g])
+                    o = dot(yz[g], diagonal(m_hi, left, right))
+                    e = dot(yz[g, 0:128], diagonal(m_lo, left, right))
+                    keep(g, o[0:64] + o[128:192] + e[0:64], o[64:128] + o[192:256] + e[64:128])
+            apart(two)
+            return carry
+
+        lax.fori_loop(0, NSI - 2, turn, 0)
+        def three():
+            for g in groups:
+                zf[g] = middle_of(g)
+        apart(three)
+        def four():
+            for g in groups:
+                zf[g] = product(yz[g, 64:128], yz[g, 192:256], zf[g])
+        apart(four)
+        def five():
+            for g in groups:
+                z_hi, z_lo = split(zf[g])
+                o = dot(two_rows(scales[g, 1:2]), diagonal(z_hi, left, right))
+                e = dot(two_rows(scales[g, 1:2]), diagonal(z_lo, left, right))
+                scales[g, 2:3] = o[0:1] + o[1:2] + e[0:1]
+        apart(five)
+        def six():
+            for g in groups:
+                z = zf[g]
+                inv = scales[g, 0:1]
+                d_hi, d_lo = split(z * scales[g, 2:3])
+                s = dot(jnp.concatenate([d_hi, d_lo], 0), ones)
+                t = z * (jnp.sqrt(K - 1.0) * jnp.sqrt(inv)) + (s[:K] + s[K:]) * inv
+                tb[2 * g] = t[:, :128].astype(BF16)
+                tb[2 * g + 1] = t[:, 128:].astype(BF16)
+        apart(six)
+
+    split_ns = 1
+    invert(range(4) if split_ns else range(8))
+
+    p0, p8, p10 = tb[0].astype(F32), tb[4].astype(F32), tb[5].astype(F32)
+    csend[0] = jnp.where(half64, p0, pltpu.roll(p8, 64, 1)).astype(BF16)
+    csend[1] = jnp.where(half64, pltpu.roll(p8, 64, 1), pltpu.roll(p10, 64, 1)).astype(BF16)
     third = [
         remote(tb.at[pl.ds(0, 4)], rrow, t_send.at[0], t_recv.at[0], (up, jb)),
         remote(csend, rcol, t_send.at[1], t_recv.at[1], (ia, west)),
@@ -289,7 +386,8 @@
     ]
     for copy in third:
         copy.start()
-
+    if split_ns:
+        invert(range(4, 8))
     zero64 = jnp.zeros((K, 128), F32)
 
     def expand(pair):
@@ -300,16 +398,16 @@
         return d0.astype(BF16), d1.astype(BF16)
 
     for m in range(16):
-        a, c = m // 4, 2 * (m % 4)
-        dd[a, c], dd[a, c + 1] = expand(tb[m])
+        for p, d in zip(ORDER[2 * m : 2 * m + 2], expand(tb[m])):
+            dd[p // 8, p % 8] = d
 
     last = ia == na - 1
     for copy in third:
         copy.wait()
     edge = last.astype(F32)
     for i in range(4):
-        mixed = rrow[i].astype(F32) * (1.0 - edge) + tb[12 + i].astype(F32) * edge
-        dd[4, 2 * i], dd[4, 2 * i + 1] = expand(mixed)
+        for c, d in zip((2 * i, 2 * i + 1), expand(rrow[i])):
+            dd[4, c] = (d.astype(F32) * (1.0 - edge) + dd[3, c].astype(F32) * edge).astype(BF16)
     for i in range(2):
         dd[2 * i, 8], dd[2 * i + 1, 8] = expand(rcol[i])
     bottom = pltpu.roll(rcol[1].astype(F32), 64, 1)
@@ -346,14 +444,22 @@
 
     def body(ensemble, channel_weights, block_column, innovation, error_precision, block_count, neighbours):
         vmem = pl.BlockSpec(memory_space=pltpu.VMEM)
-        smem = pl.BlockSpec(memory_space=pltpu.SMEM)
         dma = pltpu.SemaphoreType.DMA
         return pl.pallas_call(
             functools.partial(kernel, na, nb),
             out_shape=jax.ShapeDtypeStruct(ensemble.shape, BF16),
-            in_specs=[vmem, vmem, vmem, vmem, vmem, smem, vmem],
+            in_specs=[pl.BlockSpec(memory_space=pl.ANY)] * 7,
             out_specs=vmem,
             scratch_shapes=[
+                pltpu.VMEM(ensemble.shape, BF16),
+                pltpu.VMEM((NBLK, LEV, OB), BF16),
+                pltpu.VMEM((1, NBLK), jnp.int32),
+                pltpu.VMEM((NBLK, OB), BF16),
+                pltpu.VMEM((NBLK, OB), BF16),
+                pltpu.SMEM((1, 1), jnp.int32),
+                pltpu.VMEM((32, NNB), jnp.int32),
+                dma((7,)),
+                pltpu.VMEM((NBLK, K + 16, OB), BF16),
                 pltpu.VMEM((LEV * PAD, 128), F32),
                 pltpu.VMEM((72 * PAD, 128), F32),
                 pltpu.VMEM((2, NBLK, OB), F32),
@@ -364,7 +470,7 @@
                 pltpu.VMEM((2, NT, 32, 128), BF16),
                 pltpu.VMEM((2, NT, 32, 128), BF16),
                 pltpu.VMEM((NT, 32, 128), F32),
-                pltpu.VMEM((NT * PAD, 128), F32),
+                pltpu.VMEM((66 * PAD, 128), F32),
                 pltpu.VMEM((8, 256, 256), BF16),
                 pltpu.VMEM((8, K, 256), F32),
                 pltpu.VMEM((16, K, 128), BF16),
@@ -377,11 +483,11 @@
                 pltpu.VMEM((CLAT, 272, 128), F32),
                 pltpu.VMEM((2, 272, 128), F32),
                 pltpu.VMEM((8, 8, 256), F32),
-                dma((2,)), dma((2,)), dma((2,)), dma((2,)), dma((2,)), dma((2,)),
-                dma((2, 3)), dma((2, 3)), dma((3,)), dma((3,)),
+                dma((2, 4)), dma((2, 4)), dma((2,)), dma((2,)), dma((2,)), dma((2,)),
+                dma((2, 4)), dma((2, 4)), dma((3,)), dma((3,)),
             ],
             compiler_params=pltpu.CompilerParams(
-                collective_id=0, has_side_effects=True, vmem_limit_bytes=48 * 2**20
+                collective_id=0, has_side_effects=True, vmem_limit_bytes=60 * 2**20
             ),
         )(
             ensemble,

time: 48.4 us -> 37.5 us (0.77)
  Pallas kernels: 42.1 us -> 34.7 us
  local copies, waits for them, and re-layouts: 4.85 us -> 1.88 us
    pallas_call x1, Pallas kernels: 42.1 us -> 34.7 us  [body(): pl.pallas_call(functools.partial(kernel, na, nb), out_shape=jax.ShapeDtyp...]
    unnamed x13 -> x1, local copies, waits for them, and re-layouts: 4.85 us -> 1.88 us
where the time goes in v2:
time: 37.5 us; the launch traced here: 37.2 us
  Pallas kernels  34.7 us (93%)
  local copies, waits for them, and re-layouts  1.88 us (5%)
  between operations  0.66 us (2%)
    pallas_call x1, Pallas kernels, body(): pl.pallas_call(functools.partial(kernel, na, nb), out_shape=jax.ShapeDtyp...  34.7 us
    unnamed x1, local copies, waits for them, and re-layouts  1.88 us

profile of v2, /device:TPU:1, one launch (start us, length us, event | category | flops | bytes accessed | tf_op | source)
XLA Modules:
  0.0 37.2 jit_solution(8045055295440822578)
XLA Ops:
  0.7 34.7 %shard_map.73 = bf16[8,16,2048]{2,1,0:T(8,128)(2,1)} custom-call(bf16[8,16,2048]{2,1,0:T(8,128)(2,1)} %ens_h.1, bf16[32,32,128]{2,1,0:T(8,128)(2,1)} %bitcast.5, s32[1,32]{1,0:T(1,128)} %bitcast.9, bf16[32,128]{1,0:T(8,128)(2,1)} %bitcast.7, bf16[32,128]{1,0:T(8,128)(2,1)} %bitcast.8, s32[1,1]{1,0:T(1,128)S(6)} %copy.9.cnt_h, s32[32,12]{1,0:T(8,128)} %bitcast.6), custom_call_target="tpu_custom_call" | custom-call | tf_op jit(solution)/shard_map/pallas_call | solution.py:448
  35.3 1.9 %copy.10 = bf16[8,16,2048]{2,1,0:T(8,128)(2,1)} copy(bf16[8,16,2048]{2,1,0:T(8,128)(2,1)} %shard_map.73) | data formatting | bytes 1048576

commit v3 on v2

--- a/solution.py
+++ b/solution.py
@@ -49,14 +49,14 @@
 
 
 def kernel(
-    na, nb, ens_h, w_h, bcol_h, innov_h, prec_h, cnt_h, nbs_h, out,
-    ens, w, bcol, innov, prec, cnt, nbs, in_sem, yb, sa, sg, sp, gall, nbp, msend, mrecv, ssend, srecv, own, s2, yz, zf, tb, csend, rrow, rcol, rcor, dd, xa, sx, so,
+    na, nb, ens_h, w_h, bcol_h, innov_h, prec_h, cnt, nbs_h, out,
+    out_v, o_sem, pf, yf, ens, w, bcol, innov, prec, nbs, in_sem, yb, sa, sg, sp, gall, nbp, msend, mrecv, ssend, srecv, own, s2, zf, tb, csend, rrow, rcol, rcor, dd, xa, sx, so,
     scales, g_send, g_recv, n_send, n_recv, m_send, m_recv, s_send, s_recv, t_send, t_recv,
 ):
     loads = [
         pltpu.make_async_copy(src, dst, in_sem.at[i])
         for i, (src, dst) in enumerate(
-            ((bcol_h, bcol), (cnt_h, cnt), (ens_h, ens), (w_h, w), (prec_h, prec), (innov_h, innov), (nbs_h, nbs))
+            ((bcol_h, bcol), (ens_h, ens), (w_h, w), (prec_h, prec), (innov_h, innov), (nbs_h, nbs))
         )
     ]
     for load in loads:
@@ -259,18 +259,12 @@
         hi = x.astype(BF16).astype(F32)
         return jnp.where(row16 == 0, hi, jnp.where(row16 == 1, x - hi, 0.0)).astype(BF16)
 
-    def product(a_hi, a_lo, b):
-        b_hi, b_lo = split(b)
-        o = dot(jnp.concatenate([a_hi, a_lo], 0), diagonal(b_hi, left, right))
-        return o[:K] + o[K:] + dot(a_hi, diagonal(b_lo, left, right))
-
-    def keep(g, y, z):
-        y_hi, y_lo = split(y)
-        z_hi, z_lo = split(z)
-        yz[g, 0:64] = y_hi
-        yz[g, 64:128] = z_hi
-        yz[g, 128:192] = y_lo
-        yz[g, 192:256] = z_lo
+    def both(x):
+        return jnp.concatenate(split(x), 0)
+
+    def thrice(a, b_hi, b_lo):
+        o = dot(both(a), diagonal(b_hi, left, right))
+        return o[:K] + o[K:] + dot(a.astype(BF16), diagonal(b_lo, left, right))
 
     def symmetric(m):
         upper, own_diagonal = [], []
@@ -291,90 +285,77 @@
             q1 = s2[pl.ds(64 * PAD + 2 * m + 1, 1), :]
             proj.append(jnp.where(half1, q0, pltpu.roll(q1, 64, 1)))
         gram = jnp.concatenate(parts, 1) + (K - 1.0) * eye
-        zf[g] = gram
+        yf[g] = gram
         scales[g, 1:2] = jnp.concatenate(proj, 1)
         scales[g, 0:1] = jnp.sum(gram * gram, axis=0, keepdims=True)
 
-    def scale(g):
+    def first_step(g):
+        gram, row = yf[g], scales[g, 1:2]
         sums = dot(two_rows(scales[g, 0:1]), ones)
-        scales[g, 0:1] = 1.0 / jnp.sqrt(sums[0:1] + sums[1:2])
-
-    def first_step(g):
-        x = zf[g] * scales[g, 0:1]
-        middle = 1.5 * eye - 0.5 * x
-        x_hi, x_lo = split(x)
-        keep(g, product(x_hi, x_lo, middle), middle)
-
-    def middle_of(g):
-        z_hi, z_lo = yz[g, 64:128], yz[g, 192:256]
-        o = dot(jnp.concatenate([z_hi, z_lo], 0), diagonal(yz[g, 0:64], left, right))
-        o = o[:K] + o[K:] + dot(z_hi, diagonal(yz[g, 128:192], left, right))
-        return 1.5 * eye - 0.5 * o
-
-    SEP = 1
-    def apart(f):
-        if SEP:
-            pl.when(ia >= 0)(f)
-        else:
-            f()
-
-    def invert(groups):
-        def opening():
-            for g in groups:
-                begin(g)
-        apart(opening)
-        def scaling():
-            for g in groups:
-                scale(g)
-        apart(scaling)
-        def start():
-            for g in groups:
-                first_step(g)
-        apart(start)
-
-        def turn(step, carry):
-            def one():
-                for g in groups:
-                    zf[g] = middle_of(g)
-            apart(one)
-            def two():
-                for g in groups:
-                    m_hi, m_lo = split(zf[g])
-                    o = dot(yz[g], diagonal(m_hi, left, right))
-                    e = dot(yz[g, 0:128], diagonal(m_lo, left, right))
-                    keep(g, o[0:64] + o[128:192] + e[0:64], o[64:128] + o[192:256] + e[64:128])
-            apart(two)
-            return carry
-
-        lax.fori_loop(0, NSI - 2, turn, 0)
-        def three():
-            for g in groups:
-                zf[g] = middle_of(g)
-        apart(three)
-        def four():
-            for g in groups:
-                zf[g] = product(yz[g, 64:128], yz[g, 192:256], zf[g])
-        apart(four)
-        def five():
-            for g in groups:
-                z_hi, z_lo = split(zf[g])
-                o = dot(two_rows(scales[g, 1:2]), diagonal(z_hi, left, right))
-                e = dot(two_rows(scales[g, 1:2]), diagonal(z_lo, left, right))
-                scales[g, 2:3] = o[0:1] + o[1:2] + e[0:1]
-        apart(five)
-        def six():
-            for g in groups:
-                z = zf[g]
-                inv = scales[g, 0:1]
-                d_hi, d_lo = split(z * scales[g, 2:3])
-                s = dot(jnp.concatenate([d_hi, d_lo], 0), ones)
-                t = z * (jnp.sqrt(K - 1.0) * jnp.sqrt(inv)) + (s[:K] + s[K:]) * inv
-                tb[2 * g] = t[:, :128].astype(BF16)
-                tb[2 * g + 1] = t[:, 128:].astype(BF16)
-        apart(six)
-
-    split_ns = 1
-    invert(range(4) if split_ns else range(8))
+        g_hi = gram.astype(BF16)
+        o = dot(jnp.concatenate([g_hi, two_rows(row)], 0), diagonal(g_hi, left, right))
+        inv = 1.0 / jnp.sqrt(sums[0:1] + sums[1:2])
+        x = gram * inv
+        yf[g] = 1.5 * x - (0.5 * inv * inv) * o[:K]
+        zf[g] = 1.5 * eye - 0.5 * x
+        scales[g, 0:1] = inv
+        scales[g, 1:2] = 1.5 * row - 0.5 * inv * (o[K : K + 1] + o[K + 1 : K + 2])
+
+    def advance(g, refine, keep_y=True):
+        y, z, row, p = yf[g], zf[g], scales[g, 1:2], pf[g]
+        p_hi, p_lo = split(p)
+        top = [y.astype(BF16)] if keep_y else []
+        parts = top + [z.astype(BF16), two_rows(row)]
+        if refine:
+            parts += ([split(y)[1]] if keep_y else []) + [split(z)[1]]
+        o = dot(jnp.concatenate(parts, 0), diagonal(p_hi, left, right))
+        n = K if keep_y else 0
+        yp, zp, rp = o[:n], o[n : n + K], o[n + K : n + K + 1] + o[n + K + 1 : n + K + 2]
+        if refine:
+            m = n + K + 16
+            e = dot(jnp.concatenate(parts[: len(top) + 2], 0), diagonal(p_lo, left, right))
+            yp = yp + o[m : m + n] + e[:n]
+            zp = zp + o[m + n : m + n + K] + e[n : n + K]
+            rp = rp + e[n + K : n + K + 1]
+        if keep_y:
+            yf[g] = 1.5 * y - 0.5 * yp
+        zf[g] = 1.5 * z - 0.5 * zp
+        scales[g, 1:2] = 1.5 * row - 0.5 * rp
+
+    def refined(g):
+        pf[g] = thrice(zf[g], *split(yf[g]))
+
+    def turn(step, carry):
+        for g in range(8):
+            pf[g] = dot(zf[g].astype(BF16), diagonal(yf[g].astype(BF16), left, right))
+        for g in range(8):
+            advance(g, False)
+        return carry
+
+    R4, R5 = 1, 1
+
+    def last_turns(groups):
+        for g in groups:
+            refined(g)
+        for g in groups:
+            advance(g, R4)
+        for g in groups:
+            refined(g)
+        for g in groups:
+            advance(g, R5, False)
+        for g in groups:
+            z, inv = zf[g], scales[g, 0:1]
+            s = dot(both(z * scales[g, 1:2]), ones)
+            t = z * (jnp.sqrt(K - 1.0) * jnp.sqrt(inv)) + (s[:K] + s[K:]) * inv
+            tb[2 * g] = t[:, :128].astype(BF16)
+            tb[2 * g + 1] = t[:, 128:].astype(BF16)
+
+    for g in range(8):
+        begin(g)
+    for g in range(8):
+        first_step(g)
+    lax.fori_loop(0, NSI - 3, turn, 0)
+    last_turns(range(4))
 
     p0, p8, p10 = tb[0].astype(F32), tb[4].astype(F32), tb[5].astype(F32)
     csend[0] = jnp.where(half64, p0, pltpu.roll(p8, 64, 1)).astype(BF16)
@@ -386,8 +367,7 @@
     ]
     for copy in third:
         copy.start()
-    if split_ns:
-        invert(range(4, 8))
+    last_turns(range(4, 8))
     zero64 = jnp.zeros((K, 128), F32)
 
     def expand(pair):
@@ -401,19 +381,7 @@
         for p, d in zip(ORDER[2 * m : 2 * m + 2], expand(tb[m])):
             dd[p // 8, p % 8] = d
 
-    last = ia == na - 1
-    for copy in third:
-        copy.wait()
-    edge = last.astype(F32)
-    for i in range(4):
-        for c, d in zip((2 * i, 2 * i + 1), expand(rrow[i])):
-            dd[4, c] = (d.astype(F32) * (1.0 - edge) + dd[3, c].astype(F32) * edge).astype(BF16)
-    for i in range(2):
-        dd[2 * i, 8], dd[2 * i + 1, 8] = expand(rcol[i])
-    bottom = pltpu.roll(rcol[1].astype(F32), 64, 1)
-    dd[4, 8] = expand(rcor[...].astype(F32) * (1.0 - edge) + bottom * edge)[0]
-
-    def finish(a, carry):
+    def finish(a):
         none = jnp.zeros((16, 128), BF16)
         for c in range(8):
             base = 2 * a * CLON + 2 * c
@@ -434,31 +402,53 @@
             for t in range(16):
                 rows = so[i, pl.ds(t * 17, CLON), :] + center[CLON * t : CLON * (t + 1)]
                 out[r, :, 128 * t : 128 * (t + 1)] = rows.astype(BF16)
+
+    def drain(a):
+        return pltpu.make_async_copy(out_v.at[pl.ds(2 * a, 2)], out.at[pl.ds(2 * a, 2)], o_sem.at[a])
+
+    third[1].wait()
+    for i in range(2):
+        for p, d in zip(((0, 1), (2, 3))[i], expand(rcol[i])):
+            dd[p, 8] = d
+
+    def most(a, carry):
+        finish(a)
         return carry
 
-    lax.fori_loop(0, 4, finish, 0)
+    lax.fori_loop(0, 3, most, 0)
+    third[0].wait()
+    third[2].wait()
+    edge = (ia == na - 1).astype(F32)
+    for i in range(4):
+        for c, d in zip((2 * i, 2 * i + 1), expand(rrow[i])):
+            dd[4, c] = (d.astype(F32) * (1.0 - edge) + dd[3, c].astype(F32) * edge).astype(BF16)
+    bottom = pltpu.roll(rcol[1].astype(F32), 64, 1)
+    dd[4, 8] = expand(rcor[...].astype(F32) * (1.0 - edge) + bottom * edge)[0]
+    finish(3)
 
 
 def solution(mesh):
     na, nb = mesh.shape["lat"], mesh.shape["lon"]
 
     def body(ensemble, channel_weights, block_column, innovation, error_precision, block_count, neighbours):
-        vmem = pl.BlockSpec(memory_space=pltpu.VMEM)
         dma = pltpu.SemaphoreType.DMA
         return pl.pallas_call(
             functools.partial(kernel, na, nb),
             out_shape=jax.ShapeDtypeStruct(ensemble.shape, BF16),
-            in_specs=[pl.BlockSpec(memory_space=pl.ANY)] * 7,
-            out_specs=vmem,
+            in_specs=[pl.BlockSpec(memory_space=pltpu.SMEM if i == 5 else pltpu.HBM) for i in range(7)],
+            out_specs=pl.BlockSpec(memory_space=pltpu.VMEM),
             scratch_shapes=[
+                pltpu.VMEM(ensemble.shape, BF16),
+                dma((4,)),
+                pltpu.VMEM((8, K, 256), F32),
+                pltpu.VMEM((8, K, 256), F32),
                 pltpu.VMEM(ensemble.shape, BF16),
                 pltpu.VMEM((NBLK, LEV, OB), BF16),
                 pltpu.VMEM((1, NBLK), jnp.int32),
                 pltpu.VMEM((NBLK, OB), BF16),
                 pltpu.VMEM((NBLK, OB), BF16),
-                pltpu.SMEM((1, 1), jnp.int32),
                 pltpu.VMEM((32, NNB), jnp.int32),
-                dma((7,)),
+                dma((6,)),
                 pltpu.VMEM((NBLK, K + 16, OB), BF16),
                 pltpu.VMEM((LEV * PAD, 128), F32),
                 pltpu.VMEM((72 * PAD, 128), F32),
@@ -471,7 +461,6 @@
                 pltpu.VMEM((2, NT, 32, 128), BF16),
                 pltpu.VMEM((NT, 32, 128), F32),
                 pltpu.VMEM((66 * PAD, 128), F32),
-                pltpu.VMEM((8, 256, 256), BF16),
                 pltpu.VMEM((8, K, 256), F32),
                 pltpu.VMEM((16, K, 128), BF16),
                 pltpu.VMEM((2, K, 128), BF16),
@@ -487,16 +476,21 @@
                 dma((2, 4)), dma((2, 4)), dma((3,)), dma((3,)),
             ],
             compiler_params=pltpu.CompilerParams(
-                collective_id=0, has_side_effects=True, vmem_limit_bytes=60 * 2**20
+                collective_id=0, has_side_effects=True, vmem_limit_bytes=20 * 2**20
             ),
         )(
-            ensemble,
-            channel_weights[0, 0],
-            block_column[0],
-            innovation[0, 0],
-            error_precision[0, 0],
-            block_count,
-            neighbours.reshape(32, NNB),
+            *(
+                x if x.ndim == 2 and x.shape[1] == 1 else pltpu.with_memory_space_constraint(x, pltpu.HBM)
+                for x in (
+                    ensemble,
+                    channel_weights[0, 0],
+                    block_column[0],
+                    innovation[0, 0],
+                    error_precision[0, 0],
+                    block_count,
+                    neighbours.reshape(32, NNB),
+                )
+            )
         )
 
     return jax.shard_map(

time: 37.5 us -> 33.7 us (0.90)
  the two profiles are of different devices: /device:TPU:1 before, /device:TPU:27 now
where the time goes in v3:
time: 33.7 us; the launch traced here: 33.6 us
  Pallas kernels  32.1 us (95%)
  local copies, waits for them, and re-layouts  0.8 us (2%)
  between operations  0.66 us (2%)
    pallas_call x1, Pallas kernels, body(): pl.pallas_call(functools.partial(kernel, na, nb), out_shape=jax.ShapeDtyp...  32.1 us
    unnamed x1, local copies, waits for them, and re-layouts  0.8 us

profile of v3, /device:TPU:27, one launch (start us, length us, event | category | flops | bytes accessed | tf_op | source)
XLA Modules:
  0.0 33.6 jit_solution(8326163324080488547)
XLA Ops:
  0.7 32.1 %shard_map.73 = bf16[8,16,2048]{2,1,0:T(8,128)(2,1)S(1)} custom-call(bf16[8,16,2048]{2,1,0:T(8,128)(2,1)} %ens_h.1, bf16[32,32,128]{2,1,0:T(8,128)(2,1)} %bitcast.5, s32[1,32]{1,0:T(1,128)} %bitcast.9, bf16[32,128]{1,0:T(8,128)(2,1)} %bitcast.7, bf16[32,128]{1,0:T(8,128)(2,1)} %bitcast.8, s32[1,1]{1,0:T(1,128)S(6)} %copy.9.cnt, s32[32,12]{1,0:T(8,128)} %bitcast.6), custom_call_target="tpu_custom_call" | custom-call | tf_op jit(solution)/shard_map/pallas_call | solution.py:435
  32.8 0.8 %copy.10 = bf16[8,16,2048]{2,1,0:T(8,128)(2,1)} copy(bf16[8,16,2048]{2,1,0:T(8,128)(2,1)S(1)} %shard_map.73) | data formatting | bytes 1048576

commit v4 on v3

--- a/solution.py
+++ b/solution.py
@@ -56,7 +56,7 @@
     loads = [
         pltpu.make_async_copy(src, dst, in_sem.at[i])
         for i, (src, dst) in enumerate(
-            ((bcol_h, bcol), (ens_h, ens), (w_h, w), (prec_h, prec), (innov_h, innov), (nbs_h, nbs))
+            ((bcol_h, bcol), (ens_h, ens), (prec_h, prec), (innov_h, innov), (w_h, w), (nbs_h, nbs))
         )
     ]
     for load in loads:
@@ -65,9 +65,36 @@
     up, down = lax.rem(ia + na - 1, na), lax.rem(ia + 1, na)
     west, east = lax.rem(jb + nb - 1, nb), lax.rem(jb + 1, nb)
 
+    has_up, has_down = ia > 0, ia < na - 1
+
     barrier = pltpu.get_barrier_semaphore()
-    for peer in ((up, jb), (down, jb), (ia, west), (ia, east), (up, west), (down, east)):
-        pl.semaphore_signal(barrier, inc=1, device_id=peer, device_id_type=MESH)
+
+    def greet(peers):
+        for peer in peers:
+            pl.semaphore_signal(barrier, inc=1, device_id=peer, device_id_type=MESH)
+
+    greet(((ia, west), (ia, east)))
+    pl.when(has_up)(lambda: greet(((up, jb), (up, west))))
+    pl.when(has_down)(lambda: greet(((down, jb), (down, east))))
+
+    @pl.when(jnp.logical_not(has_up))
+    def _():
+        srecv[0] = jnp.zeros_like(srecv[0])
+        nbp[2] = jnp.zeros_like(nbp[2])
+
+    @pl.when(jnp.logical_not(has_down))
+    def _():
+        srecv[1] = jnp.zeros_like(srecv[1])
+        nbp[0] = jnp.zeros_like(nbp[0])
+        rrow[...] = jnp.zeros_like(rrow)
+        rcor[...] = jnp.zeros_like(rcor)
+
+    def each(cond, copies, what):
+        def run():
+            for copy in copies:
+                getattr(copy, what)()
+
+        pl.when(cond)(run)
 
     def remote(src, dst, send, recv, peer):
         return pltpu.make_async_remote_copy(
@@ -81,8 +108,8 @@
     lane128 = lax.broadcasted_iota(jnp.int32, (128, 128), 1)
     averager = jnp.where(row128 // 64 == lane128 // 64, 1.0 / K, 0.0).astype(BF16)
 
-    for load in loads:
-        load.wait()
+    loads[0].wait()
+    loads[1].wait()
 
     code = jnp.zeros((1, 128), jnp.int32)
     columns = jnp.concatenate([bcol[...], jnp.zeros((1, 128 - NBLK), jnp.int32)], 1)
@@ -91,8 +118,6 @@
     msend[0] = jnp.broadcast_to(code, (8, 128))
     msend[1] = jnp.broadcast_to(pltpu.roll(code, 2 * NBLK, 1), (8, 128))
     code_own = pltpu.roll(code, NBLK, 1)
-    for to, start, rows in ((0, 0, 8), (8, 8, 1), (9, 16, 1), (10, 24, 1), (11, 9, 7), (18, 17, 7), (25, 25, 7)):
-        nbp[1, to : to + rows, 0:NNB] = nbs[start : start + rows]
 
     chosen = jnp.where(row128 == jnp.broadcast_to(columns, (128, 128)), 1.0, 0.0)
     chosen = jnp.where(lane128 < NBLK, chosen, 0.0)
@@ -105,6 +130,8 @@
         part = anomaly[NBLK * t : NBLK * (t + 1)]
         sa[pl.ds(2 * t * PAD, NBLK), :] = part
         sa[pl.ds((2 * t + 1) * PAD, NBLK), :] = pltpu.roll(part, 64, 1)
+    for load in loads[2:5]:
+        load.wait()
     sp[0] = jnp.sqrt(prec[...].astype(F32))
     sp[1] = innov[...].astype(F32) * sp[0]
 
@@ -134,34 +161,44 @@
     def unit(k):
         return sg[pl.ds(k * PAD, NBLK), :]
 
-    for i in range(16):
+    def pack(i):
+        if i == 16:
+            spine = jnp.zeros((NBLK, 128), F32)
+            for k in range(32, 64):
+                spine = jnp.where(wide == k, unit(k), spine)
+            gall[1, 16] = jnp.where(wide < 64, unit(64), pltpu.roll(spine, 64, 1)).astype(BF16)
+            return
         k = i + 16
         low = unit(i) if i == 0 else jnp.where(wide >= i, unit(i), pltpu.roll(unit(63 - i), 64 + i, 1))
         high = jnp.where(wide >= 64 + k, pltpu.roll(unit(k), 64, 1), pltpu.roll(unit(63 - k), k, 1))
         gall[1, i] = jnp.where(wide < 64, low, high).astype(BF16)
-    spine = jnp.zeros((NBLK, 128), F32)
-    for k in range(32, 64):
-        spine = jnp.where(wide == k, unit(k), spine)
-    gall[1, 16] = jnp.where(wide < 64, unit(64), pltpu.roll(spine, 64, 1)).astype(BF16)
-
-    pl.semaphore_wait(barrier, 6)
+
+    loads[5].wait()
+    for to, start, rows in ((0, 0, 8), (8, 8, 1), (9, 16, 1), (10, 24, 1), (11, 9, 7), (18, 17, 7), (25, 25, 7)):
+        nbp[1, to : to + rows, 0:NNB] = nbs[start : start + rows]
+    pl.semaphore_wait(barrier, 2 + 2 * has_up.astype(jnp.int32) + 2 * has_down.astype(jnp.int32))
     facts = [
         remote(nbp.at[1], nbp.at[0], n_send.at[0], n_recv.at[0], (up, jb)),
         remote(nbp.at[1], nbp.at[2], n_send.at[1], n_recv.at[1], (down, jb)),
         remote(msend.at[0], mrecv.at[0], m_send.at[0], m_recv.at[0], (ia, east)),
         remote(msend.at[1], mrecv.at[1], m_send.at[1], m_recv.at[1], (ia, west)),
     ]
+    each(has_up, facts[:1], "start")
+    each(has_down, facts[1:2], "start")
+    for copy in facts[2:]:
+        copy.start()
+    for i in range(17):
+        pack(i)
     first = []
     for n, (lo, hi) in enumerate(CHUNKS):
         span = pl.ds(lo, hi - lo)
-        first.append(
-            [
-                remote(gall.at[1, span], gall.at[0, span], g_send.at[0, n], g_recv.at[0, n], (ia, east)),
-                remote(gall.at[1, span], gall.at[2, span], g_send.at[1, n], g_recv.at[1, n], (ia, west)),
-            ]
-        )
-    for copy in facts + [copy for pair in first for copy in pair]:
-        copy.start()
+        pair = [
+            remote(gall.at[1, span], gall.at[0, span], g_send.at[0, n], g_recv.at[0, n], (ia, east)),
+            remote(gall.at[1, span], gall.at[2, span], g_send.at[1, n], g_recv.at[1, n], (ia, west)),
+        ]
+        for copy in pair:
+            copy.start()
+        first.append(pair)
 
     def columns_of(r, carry):
         x = jnp.concatenate([ens[r, :, 128 * t : 128 * (t + 1)] for t in range(16)], 0)
@@ -174,8 +211,10 @@
 
     lax.fori_loop(0, CLAT, columns_of, 0)
 
-    for copy in facts:
-        copy.wait()
+    each(has_down, facts[:1], "wait_recv")
+    each(has_up, facts[1:2], "wait_recv")
+    for copy in facts[2:]:
+        copy.wait_recv()
     code3 = mrecv[0, 0:1, :] + code_own + mrecv[1, 0:1, :]
     is_live = (code3 > 0).astype(F32)
     place = jnp.maximum(code3 - 1, 0)
@@ -206,7 +245,7 @@
     second = []
     for n, (lo, hi) in enumerate(CHUNKS):
         for copy in first[n]:
-            copy.wait()
+            copy.wait_recv()
         for t in range(lo, hi, 2):
             ts = range(t, min(t + 2, hi))
             rhs = jnp.concatenate([jnp.concatenate([gall[v, i] for i in ts], 1) for v in range(3)], 0)
@@ -222,12 +261,12 @@
             remote(ssend.at[0, span], srecv.at[0, span], s_send.at[0, n], s_recv.at[0, n], (down, jb)),
             remote(ssend.at[1, span], srecv.at[1, span], s_send.at[1, n], s_recv.at[1, n], (up, jb)),
         ]
-        for copy in pair:
-            copy.start()
+        each(has_down, pair[:1], "start")
+        each(has_up, pair[1:], "start")
         second.append(pair)
     for n, (lo, hi) in enumerate(CHUNKS):
-        for copy in second[n]:
-            copy.wait()
+        each(has_up, second[n][:1], "wait_recv")
+        each(has_down, second[n][1:], "wait_recv")
         for i in range(lo, hi):
             tile = own[i] + srecv[0, i].astype(F32) + srecv[1, i].astype(F32)
             if i == 16:
@@ -355,19 +394,20 @@
     for g in range(8):
         first_step(g)
     lax.fori_loop(0, NSI - 3, turn, 0)
-    last_turns(range(4))
-
+    EG = 4
+    last_turns(range(EG))
+
+    third = [
+        remote(tb.at[pl.ds(0, 4)], rrow, t_send.at[0], t_recv.at[0], (up, jb)),
+        remote(csend, rcol, t_send.at[1], t_recv.at[1], (ia, west)),
+        remote(tb.at[0], rcor, t_send.at[2], t_recv.at[2], (up, west)),
+    ]
     p0, p8, p10 = tb[0].astype(F32), tb[4].astype(F32), tb[5].astype(F32)
     csend[0] = jnp.where(half64, p0, pltpu.roll(p8, 64, 1)).astype(BF16)
     csend[1] = jnp.where(half64, pltpu.roll(p8, 64, 1), pltpu.roll(p10, 64, 1)).astype(BF16)
-    third = [
-        remote(tb.at[pl.ds(0, 4)], rrow, t_send.at[0], t_recv.at[0], (up, jb)),
-        remote(csend, rcol, t_send.at[1], t_recv.at[1], (ia, west)),
-        remote(csend.at[0], rcor, t_send.at[2], t_recv.at[2], (up, west)),
-    ]
-    for copy in third:
-        copy.start()
-    last_turns(range(4, 8))
+    third[1].start()
+    each(has_up, third[::2], "start")
+    last_turns(range(EG, 8))
     zero64 = jnp.zeros((K, 128), F32)
 
     def expand(pair):
@@ -406,7 +446,7 @@
     def drain(a):
         return pltpu.make_async_copy(out_v.at[pl.ds(2 * a, 2)], out.at[pl.ds(2 * a, 2)], o_sem.at[a])
 
-    third[1].wait()
+    third[1].wait_recv()
     for i in range(2):
         for p, d in zip(((0, 1), (2, 3))[i], expand(rcol[i])):
             dd[p, 8] = d
@@ -416,8 +456,7 @@
         return carry
 
     lax.fori_loop(0, 3, most, 0)
-    third[0].wait()
-    third[2].wait()
+    each(has_down, third[::2], "wait_recv")
     edge = (ia == na - 1).astype(F32)
     for i in range(4):
         for c, d in zip((2 * i, 2 * i + 1), expand(rrow[i])):
@@ -425,6 +464,10 @@
     bottom = pltpu.roll(rcol[1].astype(F32), 64, 1)
     dd[4, 8] = expand(rcor[...].astype(F32) * (1.0 - edge) + bottom * edge)[0]
     finish(3)
+    for copy in facts[2:] + third[1:2] + [copy for pair in first for copy in pair]:
+        copy.wait_send()
+    each(has_up, facts[:1] + third[::2] + [pair[1] for pair in second], "wait_send")
+    each(has_down, facts[1:2] + [pair[0] for pair in second], "wait_send")
 
 
 def solution(mesh):
@@ -472,8 +515,8 @@
                 pltpu.VMEM((CLAT, 272, 128), F32),
                 pltpu.VMEM((2, 272, 128), F32),
                 pltpu.VMEM((8, 8, 256), F32),
-                dma((2, 4)), dma((2, 4)), dma((2,)), dma((2,)), dma((2,)), dma((2,)),
-                dma((2, 4)), dma((2, 4)), dma((3,)), dma((3,)),
+                dma((2, len(CHUNKS))), dma((2, len(CHUNKS))), dma((2,)), dma((2,)), dma((2,)), dma((2,)),
+                dma((2, len(CHUNKS))), dma((2, len(CHUNKS))), dma((3,)), dma((3,)),
             ],
             compiler_params=pltpu.CompilerParams(
                 collective_id=0, has_side_effects=True, vmem_limit_bytes=20 * 2**20

time: 33.7 us -> 33.2 us (0.985)
  the two profiles are of different devices: /device:TPU:27 before, /device:TPU:19 now
where the time goes in v4:
time: 33.2 us; the launch traced here: 33.1 us
  Pallas kernels  31.6 us (95%)
  local copies, waits for them, and re-layouts  0.8 us (2%)
  between operations  0.66 us (2%)
    pallas_call x1, Pallas kernels, body(): pl.pallas_call(functools.partial(kernel, na, nb), out_shape=jax.ShapeDtyp...  31.6 us
    unnamed x1, local copies, waits for them, and re-layouts  0.8 us

profile of v4, /device:TPU:19, one launch (start us, length us, event | category | flops | bytes accessed | tf_op | source)
XLA Modules:
  0.0 33.1 jit_solution(11417077276437887787)
XLA Ops:
  0.7 31.6 %shard_map.73 = bf16[8,16,2048]{2,1,0:T(8,128)(2,1)S(1)} custom-call(bf16[8,16,2048]{2,1,0:T(8,128)(2,1)} %ens_h.1, bf16[32,32,128]{2,1,0:T(8,128)(2,1)} %bitcast.5, s32[1,32]{1,0:T(1,128)} %bitcast.9, bf16[32,128]{1,0:T(8,128)(2,1)} %bitcast.7, bf16[32,128]{1,0:T(8,128)(2,1)} %bitcast.8, s32[1,1]{1,0:T(1,128)S(6)} %copy.9.cnt, s32[32,12]{1,0:T(8,128)} %bitcast.6), custom_call_target="tpu_custom_call" | custom-call | tf_op jit(solution)/shard_map/pallas_call | solution.py:478
  32.3 0.8 %copy.10 = bf16[8,16,2048]{2,1,0:T(8,128)(2,1)} copy(bf16[8,16,2048]{2,1,0:T(8,128)(2,1)S(1)} %shard_map.73) | data formatting | bytes 1048576

commit v5 on v4

--- a/solution.py
+++ b/solution.py
@@ -21,7 +21,7 @@
 LEV = 32
 NT = 17
 PAD = 33
-CHUNKS = ((0, 4), (4, 8), (8, 12), (12, 17))
+CHUNKS = ((0, 6), (6, 12), (12, 17))
 ORDER = (0, 1, 2, 3, 4, 5, 6, 7, 8, 16, 24, 9, 10, 11, 12, 13, 14, 15) + tuple(range(17, 24)) + tuple(range(25, 32))
 
 

time: 33.2 us -> 33.1 us (level)
  no operation moved by 1% of the time
where the time goes in v5:
time: 33.1 us; the launch traced here: 33 us
  Pallas kernels  31.5 us (95%)
  local copies, waits for them, and re-layouts  0.8 us (2%)
  between operations  0.66 us (2%)
    pallas_call x1, Pallas kernels, body(): pl.pallas_call(functools.partial(kernel, na, nb), out_shape=jax.ShapeDtyp...  31.5 us
    unnamed x1, local copies, waits for them, and re-layouts  0.8 us

profile of v5, /device:TPU:19, one launch (start us, length us, event | category | flops | bytes accessed | tf_op | source)
XLA Modules:
  0.0 33.0 jit_solution(5972685375397223636)
XLA Ops:
  0.7 31.5 %shard_map.73 = bf16[8,16,2048]{2,1,0:T(8,128)(2,1)S(1)} custom-call(bf16[8,16,2048]{2,1,0:T(8,128)(2,1)} %ens_h.1, bf16[32,32,128]{2,1,0:T(8,128)(2,1)} %bitcast.5, s32[1,32]{1,0:T(1,128)} %bitcast.9, bf16[32,128]{1,0:T(8,128)(2,1)} %bitcast.7, bf16[32,128]{1,0:T(8,128)(2,1)} %bitcast.8, s32[1,1]{1,0:T(1,128)S(6)} %copy.9.cnt, s32[32,12]{1,0:T(8,128)} %bitcast.6), custom_call_target="tpu_custom_call" | custom-call | tf_op jit(solution)/shard_map/pallas_call | solution.py:478
  32.2 0.8 %copy.10 = bf16[8,16,2048]{2,1,0:T(8,128)(2,1)} copy(bf16[8,16,2048]{2,1,0:T(8,128)(2,1)S(1)} %shard_map.73) | data formatting | bytes 1048576
